TPU v7x, 32 devices: a whole 2x2x4 slice. The times are simulated.
32 devices in a mesh: grp: 4 (over y, core), rep: 8 (over z, x).
Axes of the slice: x: 2, y: 2, z: 4, core: 2. Of those that a mesh axis runs over, the one named last changes fastest.
Arguments:
- embeddings: bfloat16 [16384, 768], P(('grp', 'rep')), may hold values from -6 to 6
- cluster_ids: int32 [16384], P(('grp', 'rep')), may hold values from 0 to 12287, as said below
- owner_bounds: int32 [32], replicated, may hold values from 0 to 12287, as said below
Outputs:
- distance: float32 [16384], P(('grp', 'rep'))
- slot_index: int32 [16384], P(('grp', 'rep'))
- centroids: bfloat16 [32, 576, 768], P(('grp', 'rep'))
Inputs may be any that keep to these rules, and one draw needn't show every extreme that they name: `cluster_ids`: in the rows of one device at most 48 rows belong to the clusters of one owner (owner o holds clusters owner_bounds[o] up to the next bound); in every draw some owner gets exactly 48 rows from every device. `owner_bounds`: owners are ordered grp first, then rep. The bounds rise from 0; each owner holds from 192 to 576 clusters, the last owner ending at 12288; some owner holds exactly 576.
All inputs are finite; a program needn't handle non-finite values.
Results may differ from a plain program's by a relative error of at most 0.004.
Values may be sent and summed in bfloat16 or wider, within the bound.
A program may use at most 128 MiB of HBM per device.

v0:
```python
import functools

import jax
import jax.numpy as jnp
from jax import lax
from jax.experimental import pallas as pl
from jax.experimental.pallas import tpu as pltpu
from jax.sharding import PartitionSpec as P

CL_DEV = 384
LANES = 128

epsilon = 1e-06
norm_floor = 0.25
MESH = pl.DeviceIdType.MESH
F32 = jnp.float32
BF16 = jnp.bfloat16
EXACT = lax.Precision.HIGHEST
NT = (((1,), (1,)), ((), ()))


def iota(shape, dim):
    return lax.broadcasted_iota(jnp.int32, shape, dim)


def ones_at(mask, kind):
    return jnp.where(mask, 1.0, 0.0).astype(kind)


def digits_dot(table, place):
    high = jnp.floor(table * (1.0 / 32.0))
    low = table - 32.0 * high
    upper = jnp.dot(high.astype(BF16), place, preferred_element_type=F32)
    lower = jnp.dot(low.astype(BF16), place, preferred_element_type=F32)
    return 32.0 * upper + lower


def kernel(
    groups, replicas, direct, extra,
    emb_ref, ids_ref, bounds_ref,
    cent_ref, dist_ref, rank_ref, over_ref,
    unit, send_rows, got_rows, send_ids, got_ids, member, total, ret, got_ret, slot_mat,
    row_send, row_recv, id_send, id_recv, ret_send, ret_recv,
    near_send, near_recv, far_send, far_recv,
):
    my_group = lax.axis_index("grp")
    my_replica = lax.axis_index("rep")
    me = my_group * replicas + my_replica
    owners = groups * replicas
    rows, width = emb_ref.shape
    limit = cent_ref.shape[0]
    slots = direct + extra
    block = replicas * slots
    sent = replicas * direct

    def peer(dg, dr):
        return lax.rem(my_group + dg, groups), lax.rem(my_replica + dr, replicas)

    def source(dg, dr):
        return (
            lax.rem(my_group + groups - dg, groups),
            lax.rem(my_replica + replicas - dr, replicas),
        )

    def every(dg, act):
        def one(dr, carry):
            act(dr)
            return carry

        lax.fori_loop(1 if dg == 0 else 0, replicas, one, 0)

    def copy(src, dst, ssem, rsem, pair, here, there):
        return pltpu.make_async_remote_copy(
            src_ref=src.at[there],
            dst_ref=dst.at[here, pl.ds(0, direct)] if dst is got_rows else dst.at[here],
            send_sem=ssem.at[there],
            recv_sem=rsem.at[here],
            device_id=pair,
            device_id_type=MESH,
        )

    def start(bufs, dg, dr):
        pair = peer(dg, dr)
        copy(*bufs, pair, me, pair[0] * replicas + pair[1]).start()

    def wait_send(bufs, dg, dr):
        pair = peer(dg, dr)
        copy(*bufs, pair, me, pair[0] * replicas + pair[1]).wait_send()

    def wait_recv(bufs, dg, dr):
        pair = source(dg, dr)
        there = pair[0] * replicas + pair[1]
        copy(*bufs, pair, there, there).wait_recv()

    row_bufs = (send_rows, got_rows, row_send, row_recv)
    id_bufs = (send_ids, got_ids, id_send, id_recv)
    ret_bufs = (ret, got_ret, ret_send, ret_recv)
    order = list(range(1, groups)) + [0]

    barrier = pltpu.get_barrier_semaphore()
    for dg in order:
        every(
            dg,
            lambda dr, dg=dg: pl.semaphore_signal(
                barrier, inc=1, device_id=peer(dg, dr), device_id_type=MESH
            ),
        )

    ids = ids_ref[...]
    edges = bounds_ref[...]
    reached = ones_at(edges <= ids, F32)
    owner = jnp.sum(reached, axis=0, keepdims=True).astype(jnp.int32) - 1
    owned = iota((owners, rows), 0) == owner
    owned_f = ones_at(owned, F32)
    first = jnp.sum(owned_f * edges.astype(F32), axis=0, keepdims=True)
    local = ids.astype(F32) - first
    earlier = ones_at(iota((rows, rows), 0) < iota((rows, rows), 1), BF16)
    prefix = jnp.dot(owned_f.astype(BF16), earlier, preferred_element_type=F32)
    rank = jnp.sum(owned_f * prefix, axis=0, keepdims=True).astype(jnp.int32)
    target = jnp.where(rank < direct, owner * direct + rank, -1)
    spot = rank
    if extra:
        late = ones_at(rank >= direct, F32)
        queue = jnp.dot(
            jnp.broadcast_to(late, (8, rows)).astype(BF16), earlier, preferred_element_type=F32
        )[0:1, :].astype(jnp.int32)
        spot = jnp.where(rank < direct, rank, direct + queue)
    place = ones_at(iota((LANES, rows), 0) == spot, BF16)

    values = emb_ref[...].astype(F32)
    unit[...] = (
        values * lax.rsqrt(jnp.sum(values * values, axis=1, keepdims=True) + epsilon)
    ).astype(BF16)

    def pack(dg):
        tg = lax.rem(my_group + dg, groups)
        pick = ones_at(iota((sent, rows), 0) + tg * sent == target, BF16)
        packed = jnp.dot(pick, unit[...], preferred_element_type=F32).astype(BF16)
        send_rows[pl.ds(tg * replicas, replicas)] = packed.reshape(replicas, direct, width)

    def near_copy(pair, owner_at, dr):
        ref = got_rows.at[owner_at, pl.ds(direct, extra)]
        return pltpu.make_async_remote_copy(
            src_ref=ref, dst_ref=ref, send_sem=near_send.at[dr], recv_sem=near_recv.at[dr],
            device_id=pair, device_id_type=MESH,
        )

    def far_copy(group_at, to_group, dg):
        ref = got_rows.at[pl.ds(group_at * replicas, replicas), pl.ds(direct, extra)]
        return pltpu.make_async_remote_copy(
            src_ref=ref, dst_ref=ref, send_sem=far_send.at[dg], recv_sem=far_recv.at[dg],
            device_id=(to_group, my_replica), device_id_type=MESH,
        )

    if extra:
        pick = ones_at(iota((extra, rows), 0) + direct == spot, BF16)
        got_rows[me, direct:slots] = jnp.dot(
            pick, unit[...], preferred_element_type=F32
        ).astype(BF16)
    pack(order[0])
    pl.semaphore_wait(barrier, owners - 1)
    if extra:
        every(0, lambda dr: near_copy(peer(0, dr), me, dr).start())
    every(order[0], lambda dr: start(row_bufs, order[0], dr))

    high = jnp.floor(local * (1.0 / 32.0))
    low = local - 32.0 * high
    owned_d = jnp.where(rank < direct, owned_f, 0.0)
    upper = lax.dot_general((owned_d * high).astype(BF16), place, NT, preferred_element_type=F32)
    lower = lax.dot_general((owned_d * low).astype(BF16), place, NT, preferred_element_type=F32)
    filled = lax.dot_general(owned_d.astype(BF16), place, NT, preferred_element_type=F32)
    id_table = 32.0 * upper + lower + filled - 1.0
    count = jnp.zeros((1, 1), F32)
    if extra:
        named = jnp.broadcast_to(late * (ids.astype(F32) + 1.0), (8, rows))
        others = lax.dot_general(
            named, place.astype(F32), NT, precision=EXACT, preferred_element_type=F32
        )
        id_table = id_table + others[0:1, :]
        count = jnp.sum(late, axis=1, keepdims=True)
    top = iota((8, LANES), 0) == 0
    for o in range(owners):
        send_ids[o] = jnp.where(top, id_table[o : o + 1, :], count)
    got_ids[me] = send_ids[me]

    for dg in order:
        every(dg, lambda dr, dg=dg: start(id_bufs, dg, dr))
    for dg in order[1:]:
        pack(dg)
        every(dg, lambda dr, dg=dg: start(row_bufs, dg, dr))
    got_rows[me, 0:direct] = send_rows[me]
    if extra:
        def near_wait(dr):
            pair = source(0, dr)
            near_copy(pair, pair[0] * replicas + pair[1], dr).wait_recv()

        every(0, near_wait)
        for dg in order[:-1]:
            far_copy(my_group, lax.rem(my_group + dg, groups), dg).start()

    for dg in order:
        every(dg, lambda dr, dg=dg: wait_recv(id_bufs, dg, dr))
    worst = jnp.max(got_ids[:, 1, :], axis=0, keepdims=True)
    over_ref[...] = jnp.where(worst > extra, 1, 0)
    begin = jnp.sum(
        jnp.where(iota((owners, 1), 0) == me, edges, 0), axis=0, keepdims=True
    ).astype(F32)
    ending = jnp.sum(
        jnp.where(iota((owners, 1), 0) == me + 1, edges, 0), axis=0, keepdims=True
    ).astype(F32) + jnp.where(me == owners - 1, float(CL_DEV * owners), 0.0)

    lane = iota((1, block), 1)
    quotient = jnp.zeros((1, block), jnp.int32)
    for s in range(1, replicas):
        quotient = quotient + jnp.where(lane >= s * slots, 1, 0)
    remainder = lane - quotient * slots
    spread = iota((LANES, block), 0) == remainder
    spread_b, spread_f = ones_at(spread, BF16), ones_at(spread, F32)
    from_source = ones_at(iota((replicas, block), 0) == quotient, F32)
    before = ones_at(iota((block, block), 0) < iota((block, block), 1), BF16)
    cluster = iota((limit, block), 0)

    seen = jnp.zeros((limit, 1), F32)
    for sg in range(groups):
        table = got_ids[sg * replicas : (sg + 1) * replicas, 0, :]
        if extra:
            mine = jnp.where((table >= begin) & (table < ending), table - begin, -1.0)
            table = jnp.where(iota((replicas, LANES), 1) < direct, table, mine)
        flat = jnp.sum(from_source * digits_dot(table, spread_b), axis=0, keepdims=True)
        mask = ones_at(cluster == flat.astype(jnp.int32), F32)
        mask_b = mask.astype(BF16)
        member[sg] = mask_b
        ahead = jnp.dot(mask_b, before, preferred_element_type=F32) + seen
        slot = jnp.sum(mask * ahead, axis=0, keepdims=True)
        seen = seen + jnp.sum(mask, axis=1, keepdims=True)
        slot_mat[sg] = lax.dot_general(
            from_source * slot, spread_f, NT, precision=EXACT, preferred_element_type=F32
        )
    total[...] = jnp.zeros_like(total)
    for dg in order:
        sg = lax.rem(my_group + groups - dg, groups)
        every(dg, lambda dr, dg=dg: wait_recv(row_bufs, dg, dr))
        if extra and dg:
            far_copy(sg, sg, dg).wait_recv()
        block_rows = got_rows[pl.ds(sg * replicas, replicas)].reshape(block, width)
        total[...] += jnp.dot(member[sg], block_rows, preferred_element_type=F32)

    centroid = total[...] / jnp.maximum(seen, 1.0)
    norm = jnp.sqrt(jnp.sum(centroid * centroid, axis=1, keepdims=True))
    cent_ref[...] = (centroid / jnp.maximum(norm, norm_floor)).astype(BF16)

    for dg in order:
        sg = lax.rem(my_group + groups - dg, groups)
        tg = lax.rem(my_group + groups - dg, groups)
        block_rows = got_rows[pl.ds(sg * replicas, replicas)].reshape(block, width)
        score = lax.dot_general(cent_ref[...], block_rows, NT, preferred_element_type=F32)
        near = jnp.sum(member[sg].astype(F32) * score, axis=0, keepdims=True)
        dist_mat = lax.dot_general(
            from_source * (1.0 - near), spread_f, NT, precision=EXACT, preferred_element_type=F32
        )
        rank_mat = slot_mat[sg]
        for s in range(replicas):
            ret[tg * replicas + s] = jnp.where(top, dist_mat[s : s + 1, :], rank_mat[s : s + 1, :])
        back = (groups - dg) % groups
        every(back, lambda dr, back=back: start(ret_bufs, back, dr))
    got_ret[me] = ret[me]

    place_f = ones_at(iota((LANES, rows), 0) == spot, F32)
    for dg in order:
        every(dg, lambda dr, dg=dg: wait_recv(ret_bufs, dg, dr))
    dist_all = jnp.dot(got_ret[:, 0, :], place_f, precision=EXACT, preferred_element_type=F32)
    rank_all = jnp.dot(got_ret[:, 1, :], place_f, precision=EXACT, preferred_element_type=F32)
    dist_ref[...] = jnp.sum(owned_f * dist_all, axis=0, keepdims=True)
    rank_ref[...] = jnp.sum(owned_f * rank_all, axis=0, keepdims=True).astype(jnp.int32)
    for bufs in (id_bufs, row_bufs, ret_bufs):
        for dg in order:
            every(dg, lambda dr, dg=dg, bufs=bufs: wait_send(bufs, dg, dr))
    if extra:
        every(0, lambda dr: near_copy(peer(0, dr), me, dr).wait_send())
        for dg in order[:-1]:
            far_copy(my_group, lax.rem(my_group + dg, groups), dg).wait_send()


def solution(mesh):
    groups, replicas = mesh.shape["grp"], mesh.shape["rep"]
    owners = groups * replicas

    def shards(embeddings, cluster_ids, owner_bounds):
        rows, width = embeddings.shape
        limit = CL_DEV + CL_DEV // 2
        most = -(-(3 * rows // owners) // 16) * 16
        direct = -(-2 * most // 48) * 16
        vmem = pl.BlockSpec(memory_space=pltpu.VMEM)
        small = pltpu.VMEM((owners, 8, LANES), F32)
        each = pltpu.SemaphoreType.DMA((owners,))
        near = pltpu.SemaphoreType.DMA((replicas,))
        far = pltpu.SemaphoreType.DMA((groups,))
        ids_row, edges = cluster_ids.reshape(1, rows), owner_bounds.reshape(owners, 1)

        def run(direct, extra, number):
            slots = direct + extra
            return pl.pallas_call(
                functools.partial(kernel, groups, replicas, direct, extra),
                out_shape=(
                    jax.ShapeDtypeStruct((limit, width), BF16),
                    jax.ShapeDtypeStruct((1, rows), F32),
                    jax.ShapeDtypeStruct((1, rows), jnp.int32),
                    jax.ShapeDtypeStruct((1, LANES), jnp.int32),
                ),
                in_specs=[vmem] * 3,
                out_specs=(vmem,) * 4,
                scratch_shapes=[
                    pltpu.VMEM((rows, width), BF16),
                    pltpu.VMEM((owners, direct, width), BF16),
                    pltpu.VMEM((owners, slots, width), BF16),
                    small,
                    small,
                    pltpu.VMEM((groups, limit, replicas * slots), BF16),
                    pltpu.VMEM((limit, width), F32),
                    small,
                    small,
                    pltpu.VMEM((groups, replicas, LANES), F32),
                    each, each, each, each, each, each, near, near, far, far,
                ],
                compiler_params=pltpu.CompilerParams(
                    collective_id=number,
                    has_side_effects=True,
                    vmem_limit_bytes=48 * 1024 * 1024,
                ),
            )(embeddings, ids_row, edges)

        if direct >= most:
            centroids, distance, rank, _ = run(most, 0, 0)
        else:
            first = run(direct, most - direct, 0)
            centroids, distance, rank = lax.cond(
                first[3][0, 0] > 0, lambda: run(most, 0, 1)[:3], lambda: first[:3]
            )
        return distance.reshape(rows), rank.reshape(rows), centroids[None]

    placed = (P(("grp", "rep"), None), P(("grp", "rep")), P())
    return jax.shard_map(
        shards,
        mesh=mesh,
        in_specs=placed,
        out_specs=(P(("grp", "rep")), P(("grp", "rep")), P(("grp", "rep"), None, None)),
        check_vma=False,
    )
```

profile of v0, /device:TPU:0, one launch (start us, length us, event | category | flops | bytes accessed | tf_op | source)
XLA Modules:
  0.0 68.4 jit_solution(12046658884333103642)
XLA Ops:
  0.6 0.0 copy-start
  0.6 0.8 %copy.6.bounds_ref = s32[32,1]{1,0:T(8,128)S(1)} copy(s32[32,1]{0,1:T(1,128)} %bitcast.15) | data formatting | bytes 256 | tf_op jit(solution)/shard_map/reshape | solution.py:298
  1.5 64.1 %shard_map.58 = (bf16[576,768]{1,0:T(8,128)(2,1)S(1)}, f32[1,512]{1,0:T(1,128)S(1)}, s32[1,512]{1,0:T(1,128)S(1)}, s32[1,128]{1,0:T(1,128)S(1)}) custom-call(bf16[512,768]{1,0:T(8,128)(2,1)} %emb_ref.1, s32[1,512]{1,0:T(1,128)} %bitcast.13, s32[32,1]{1,0:T(8,128)S(1)} %copy.6.bounds_ref), custom_call_target="tpu_custom_call" | custom-call | tf_op jit(solution)/shard_map/pallas_call | solution.py:302
  65.6 0.0 copy-start.1
  65.6 0.0 copy-start.2
  65.7 0.0 copy-done
  65.7 0.7 copy-done.1
  66.3 0.0 copy-done.2
  66.3 0.6 copy.20
  66.9 0.6 copy.21
  67.5 0.9 %copy.22 = bf16[1,576,768]{2,1,0:T(8,128)(2,1)} copy(bf16[1,576,768]{2,1,0:T(8,128)(2,1)S(1)} %get-tuple-element.76) | data formatting | bytes 1769472
  (1 shorter events, 0.0 us)
Async XLA Ops:
  0.6 65.0 %copy-start = (bf16[512,768]{1,0:T(8,128)(2,1)S(1)}, bf16[512,768]{1,0:T(8,128)(2,1)}, u32[]{:S(2)}) copy-start(bf16[512,768]{1,0:T(8,128)(2,1)} %emb_ref.1) | copy-start | bytes 2359300
  65.6 0.7 %copy-start.1 = (s32[512]{0:T(512)S(1)}, s32[512]{0:T(512)}, u32[]{:S(2)}) copy-start(s32[512]{0:T(512)} %param.6) | copy-start | bytes 6148
  65.6 0.7 copy-start.2
where the time goes:
time: 68.6 us; the launch traced here: 68.4 us
  Pallas kernels  64.1 us (93%)
  local copies, waits for them, and re-layouts  3.55 us (5%)
  between operations  0.71 us (1%)
    pallas_call x1, Pallas kernels, run(): pl.pallas_call(functools.partial(kernel, groups, replicas, direct, extra)...  64.1 us
    unnamed x9, local copies, waits for them, and re-layouts  2.74 us

commit v1 on v0

--- a/solution.py
+++ b/solution.py
@@ -281,6 +281,402 @@
             far_copy(my_group, lax.rem(my_group + dg, groups), dg).wait_send()
 
 
+def fold(count, size):
+    return jnp.floor((iota((1, count), 1).astype(F32) + 0.5) * (1.0 / size)).astype(jnp.int32)
+
+
+def split(value):
+    upper = value.astype(BF16)
+    return upper, (value - upper.astype(F32)).astype(BF16)
+
+
+def digits(value):
+    upper = jnp.floor(value * (1.0 / 256.0))
+    return upper.astype(BF16), (value - 256.0 * upper).astype(BF16)
+
+
+def dot(left, right):
+    return jnp.dot(left, right, preferred_element_type=F32)
+
+
+def dot_nt(left, right):
+    return lax.dot_general(left, right, NT, preferred_element_type=F32)
+
+
+def fast_kernel(
+    groups, replicas, direct, shared, spare,
+    emb_ref, ids_ref, bounds_ref,
+    cent_ref, dist_ref, rank_ref, over_ref,
+    unit, send_d, send_q, got_d, got_q, got_e,
+    send_ids, got_ids, send_rank, got_rank, send_dist, got_dist,
+    mask_d, mask_q, mask_e, total, ranks, spread,
+    d_send, d_recv, id_send, id_recv, rank_send, rank_recv, dist_send, dist_recv,
+    q_send, q_recv, qf_send, qf_recv, e_send, e_recv, ef_send, ef_recv,
+):
+    my_group = lax.axis_index("grp")
+    my_replica = lax.axis_index("rep")
+    me = my_group * replicas + my_replica
+    owners = groups * replicas
+    rows, width = emb_ref.shape
+    limit = cent_ref.shape[0]
+    planes, sides = replicas // 2, groups // 2
+    my_plane, my_col = lax.div(my_replica, 2), lax.rem(my_replica, 2)
+    my_side, my_core = lax.div(my_group, 2), lax.rem(my_group, 2)
+
+    def turn(at, step, size):
+        return lax.rem(at + step, size)
+
+    def back(at, step, size):
+        return lax.rem(at + (size - step), size)
+
+    to_group = [turn(my_group, s, groups) for s in range(groups)]
+    to_replica = [turn(my_replica, s, replicas) for s in range(replicas)]
+    from_group = [back(my_group, s, groups) for s in range(groups)]
+    from_replica = [back(my_replica, s, replicas) for s in range(replicas)]
+    steps = [
+        (dg, dr) for dg in range(groups) for dr in range(replicas) if dg or dr
+    ]
+
+    barrier = pltpu.get_barrier_semaphore()
+    for dg, dr in steps:
+        pl.semaphore_signal(
+            barrier, inc=1, device_id=(to_group[dg], to_replica[dr]), device_id_type=MESH
+        )
+
+    def remote(src, dst, ssem, rsem, pair):
+        return pltpu.make_async_remote_copy(
+            src_ref=src, dst_ref=dst, send_sem=ssem, recv_sem=rsem,
+            device_id=pair, device_id_type=MESH,
+        )
+
+    def pair_out(bufs, dg, dr):
+        src, dst, ssem, rsem = bufs
+        pair = (to_group[dg], to_replica[dr])
+        there = pair[0] * replicas + pair[1]
+        return remote(src.at[there], dst.at[me], ssem.at[there], rsem.at[me], pair)
+
+    def pair_in(bufs, dg, dr):
+        src, dst, ssem, rsem = bufs
+        pair = (from_group[dg], from_replica[dr])
+        there = pair[0] * replicas + pair[1]
+        return remote(src.at[there], dst.at[there], ssem.at[there], rsem.at[there], pair)
+
+    d_bufs = (send_d, got_d, d_send, d_recv)
+    id_bufs = (send_ids, got_ids, id_send, id_recv)
+    rank_bufs = (send_rank, got_rank, rank_send, rank_recv)
+    dist_bufs = (send_dist, got_dist, dist_send, dist_recv)
+
+    def q_out(dr):
+        there = to_replica[dr]
+        return remote(
+            send_q.at[there], got_q.at[my_group, my_replica],
+            q_send.at[dr], q_recv.at[dr], (my_group, there),
+        )
+
+    def q_in(dr):
+        there = from_replica[dr]
+        return remote(
+            send_q.at[there], got_q.at[my_group, there],
+            q_send.at[dr], q_recv.at[dr], (my_group, there),
+        )
+
+    sibling = (my_side * 2 + (1 - my_core), my_replica)
+
+    def side_pair(ds, inward):
+        side = back(my_side, ds, sides) if inward else turn(my_side, ds, sides)
+        return (side * 2 + my_core, my_replica)
+
+    def qf_side(ds, inward):
+        pair = side_pair(ds, inward)
+        group = pair[0] if inward else my_group
+        ref = got_q.at[group]
+        return remote(ref, ref, qf_send.at[ds], qf_recv.at[ds], pair)
+
+    def qf_core(ds, inward):
+        group = side_pair(ds, True)[0]
+        group = group + (1 - 2 * my_core) if inward else group
+        ref = got_q.at[group]
+        return remote(ref, ref, qf_send.at[sides + ds], qf_recv.at[sides + ds], sibling)
+
+    def e_plane(dp, inward):
+        plane = back(my_plane, dp, planes) if inward else turn(my_plane, dp, planes)
+        ref = got_e.at[my_group, my_col, plane if inward else my_plane]
+        return remote(
+            ref, ref, e_send.at[dp], e_recv.at[dp], (my_group, plane * 2 + my_col)
+        )
+
+    def e_spot(ds, dc, inward):
+        side = back(my_side, ds, sides) if inward else turn(my_side, ds, sides)
+        col = lax.rem(my_col + dc, 2)
+        return side * 2 + my_core, col
+
+    def ef_side(ds, dc, inward):
+        group, col = e_spot(ds, dc, inward)
+        ref = got_e.at[group, col] if inward else got_e.at[my_group, my_col]
+        at = ds * 2 + dc
+        return remote(
+            ref, ref, ef_send.at[at], ef_recv.at[at], (group, my_plane * 2 + col)
+        )
+
+    def ef_core(ds, dc, inward):
+        group, col = e_spot(ds, dc, True)
+        group = group + (1 - 2 * my_core) if inward else group
+        ref = got_e.at[group, col]
+        at = groups + ds * 2 + dc
+        return remote(ref, ref, ef_send.at[at], ef_recv.at[at], sibling)
+
+    ids = ids_ref[...]
+    bounds = bounds_ref[...]
+    diagonal = iota((owners, owners), 0) == iota((owners, owners), 1)
+    edges = jnp.sum(jnp.where(diagonal, bounds, 0), axis=1, keepdims=True)
+    owner = jnp.sum(ones_at(edges <= ids, F32), axis=0, keepdims=True).astype(jnp.int32) - 1
+    owned = iota((owners, rows), 0) == owner
+    owned_f = ones_at(owned, F32)
+    earlier = ones_at(iota((rows, rows), 0) < iota((rows, rows), 1), BF16)
+    prefix = dot(owned_f.astype(BF16), earlier)
+    rank = jnp.sum(owned_f * prefix, axis=0, keepdims=True).astype(jnp.int32)
+    column = lax.rem(owner, replicas)
+    in_column = iota((replicas, rows), 0) == column
+    late = rank >= direct
+    column_f = ones_at(in_column, F32)
+    late_f = jnp.where(late, column_f, 0.0)
+    column_rank = jnp.sum(
+        column_f * dot(late_f.astype(BF16), earlier), axis=0, keepdims=True
+    ).astype(jnp.int32)
+    in_direct = rank < direct
+    in_shared = jnp.logical_and(late, column_rank < shared)
+    in_spare = jnp.logical_and(late, column_rank >= shared)
+    spare_f = ones_at(in_spare, F32)
+    spare_rank = dot(
+        jnp.broadcast_to(spare_f, (8, rows)).astype(BF16), earlier
+    )[0:1, :].astype(jnp.int32)
+    count = jnp.sum(spare_f, axis=1, keepdims=True)
+
+    values = emb_ref[...].astype(F32)
+    unit[...] = (
+        values * lax.rsqrt(jnp.sum(values * values, axis=1, keepdims=True) + epsilon)
+    ).astype(BF16)
+
+    def picked(number, target):
+        return dot(ones_at(iota((number, rows), 0) == target, BF16), unit[...]).astype(BF16)
+
+    own_spare = picked(spare, jnp.where(in_spare, spare_rank, -1))
+    got_e[my_group, my_col, my_plane] = own_spare
+    packed = picked(replicas * shared, jnp.where(in_shared, column * shared + column_rank, -1))
+    send_q[...] = packed.reshape(replicas, shared, width)
+    got_q[my_group, my_replica] = send_q[my_replica]
+
+    lane = jnp.where(
+        in_direct, rank, jnp.where(in_shared, direct + column_rank, direct + shared + spare_rank)
+    )
+    place = ones_at(iota((LANES, rows), 0) == lane, BF16)
+    near_f = jnp.concatenate([column_f] * groups, axis=0)
+    chosen = jnp.where(in_direct, owned_f, jnp.where(in_shared, near_f, 1.0))
+    id_high = jnp.floor(ids.astype(F32) * (1.0 / 256.0))
+    id_low = ids.astype(F32) - 256.0 * id_high
+    used = direct + shared + spare
+    three = jnp.concatenate([chosen * id_high, chosen * id_low, chosen], axis=0).astype(BF16)
+    table = dot_nt(three, place)
+    table = 256.0 * table[0:owners] + table[owners : 2 * owners] + table[2 * owners :] - 1.0
+    table = jnp.where(iota((owners, LANES), 1) < used, table, count)
+    send_ids[...] = table.reshape(owners, 1, LANES)
+    got_ids[me] = send_ids[me]
+
+    pl.semaphore_wait(barrier, owners - 1)
+    for dp in range(1, planes):
+        e_plane(dp, False).start()
+    for dr in range(1, replicas):
+        q_out(dr).start()
+    for dg, dr in steps:
+        pair_out(id_bufs, dg, dr).start()
+
+    target = jnp.where(in_direct, owner * direct + rank, -1)
+    block = replicas * direct
+    for dg in list(range(1, groups)) + [0]:
+        tg = to_group[dg]
+        packed = picked(block, target - tg * block)
+        send_d[pl.ds(tg * replicas, replicas)] = packed.reshape(replicas, direct, width)
+        for dr in range(replicas):
+            if dg or dr:
+                pair_out(d_bufs, dg, dr).start()
+    got_d[me] = send_d[me]
+
+    for dp in range(1, planes):
+        e_plane(dp, True).wait_recv()
+    others = [(ds, dc) for ds in range(sides) for dc in range(2) if ds or dc]
+    for ds, dc in others:
+        ef_side(ds, dc, False).start()
+    ef_core(0, 0, False).start()
+    for dr in range(1, replicas):
+        q_in(dr).wait_recv()
+    for ds in range(1, sides):
+        qf_side(ds, False).start()
+    qf_core(0, False).start()
+
+    direct_row, shared_row, spare_row = groups * block, owners * shared, owners * spare
+    d_lane, q_lane, e_lane = fold(block, direct), fold(block, shared), fold(replicas * spare, spare)
+    e_col = fold(replicas * spare, spare * planes)
+    e_source = (e_lane - e_col * planes) * 2 + e_col
+    d_slot = iota((1, block), 1) - d_lane * direct
+    q_slot = iota((1, block), 1) - q_lane * shared + direct
+    e_slot = iota((1, replicas * spare), 1) - e_lane * spare + (direct + shared)
+    lane_source = jnp.concatenate([d_lane, q_lane, e_source], axis=1)
+    lane_slot = jnp.concatenate([d_slot, q_slot, e_slot], axis=1)
+    span = lane_source.shape[1]
+    expand = ones_at(iota((LANES, span), 0) == lane_slot, BF16)
+    from_source = ones_at(iota((replicas, span), 0) == lane_source, F32)
+    key = lane_source * used + lane_slot
+    key_col = jnp.sum(
+        jnp.where(iota((span, span), 0) == iota((span, span), 1), key, 0), axis=1, keepdims=True
+    )
+    before = ones_at(key_col < key, BF16)
+
+    def spread_rows(size, offset):
+        at = jnp.floor((iota((size, LANES), 0).astype(F32) + 0.5) * (1.0 / offset[0]))
+        slot = iota((size, LANES), 0) - at.astype(jnp.int32) * offset[0] + offset[1]
+        return ones_at(slot == iota((size, LANES), 1), BF16)
+
+    spread[0:direct_row] = spread_rows(direct_row, (direct, 0))
+    spread[direct_row : direct_row + shared_row] = spread_rows(shared_row, (shared, direct))
+    spread[direct_row + shared_row :] = spread_rows(spare_row, (spare, direct + shared))
+
+    d_all = fold(direct_row, direct)
+    q_all = fold(shared_row, shared)
+    e_all = fold(spare_row, spare)
+    e_group = fold(spare_row, replicas * spare)
+    e_inner = e_all - e_group * replicas
+    e_side = fold(spare_row, planes * spare) - e_group * 2
+    e_all = e_group * replicas + (e_inner - e_side * planes) * 2 + e_side
+    all_source = jnp.concatenate([d_all, q_all, e_all], axis=1)
+
+    def by_source(row, parts):
+        held = jnp.where(iota((owners, row.shape[1]), 0) == all_source, row, 0.0)
+        upper, lower = parts(held)
+        both = dot(jnp.concatenate([upper, lower], axis=0), spread[...])
+        return both[0:owners], both[owners:]
+
+    for dg, dr in steps:
+        pair_in(id_bufs, dg, dr).wait_recv()
+    named = got_ids[...].reshape(owners, LANES)
+    worst = jnp.max(named, axis=0, keepdims=True)
+    over_ref[...] = jnp.where(worst > spare, 1, 0)
+    begin = jnp.sum(jnp.where(iota((owners, 1), 0) == me, edges, 0), axis=0, keepdims=True)
+    ending = jnp.sum(
+        jnp.where(iota((owners, 1), 0) == me + 1, edges, 0), axis=0, keepdims=True
+    ) + jnp.where(me == owners - 1, CL_DEV * owners, 0)
+    begin, ending = begin.astype(F32), ending.astype(F32)
+    mine = jnp.logical_and(named >= begin, named < ending)
+    local = jnp.where(mine, named - begin + 1.0, 0.0)
+    local_high, local_low = digits(local)
+    flat_both = dot(jnp.concatenate([local_high, local_low], axis=0), expand)
+    flat_all = 256.0 * flat_both[0:owners] + flat_both[owners:] - 1.0
+
+    seen = jnp.zeros((limit, 1), F32)
+    cluster = iota((limit, span), 0)
+    wide = replicas * spare
+    for sg in range(groups):
+        flat = jnp.sum(
+            from_source * flat_all[sg * replicas : (sg + 1) * replicas], axis=0, keepdims=True
+        )
+        mask = ones_at(cluster == flat.astype(jnp.int32), F32)
+        mask_b = mask.astype(BF16)
+        mask_d[:, sg * block : (sg + 1) * block] = mask_b[:, 0:block]
+        mask_q[:, sg * block : (sg + 1) * block] = mask_b[:, block : 2 * block]
+        mask_e[:, sg * wide : (sg + 1) * wide] = mask_b[:, 2 * block :]
+        ahead = dot(mask_b, before) + seen
+        slot = jnp.sum(mask * ahead, axis=0, keepdims=True)
+        ranks[:, sg * block : (sg + 1) * block] = slot[:, 0:block]
+        at = direct_row + sg * block
+        ranks[:, at : at + block] = slot[:, block : 2 * block]
+        at = direct_row + shared_row + sg * wide
+        ranks[:, at : at + wide] = slot[:, 2 * block :]
+        seen = seen + jnp.sum(mask, axis=1, keepdims=True)
+
+    upper, lower = by_source(ranks[...], digits)
+    send_rank[...] = (256.0 * upper + lower).reshape(owners, 1, LANES)
+    got_rank[me] = send_rank[me]
+    for dg, dr in steps:
+        pair_out(rank_bufs, dg, dr).start()
+
+    for ds in range(1, sides):
+        qf_side(ds, True).wait_recv()
+        qf_core(ds, False).start()
+    for ds, dc in others:
+        ef_side(ds, dc, True).wait_recv()
+        ef_core(ds, dc, False).start()
+
+    for ds in range(sides):
+        qf_core(ds, True).wait_recv()
+    rows_q = got_q[...].reshape(shared_row, width)
+    total[...] = dot(mask_q[...], rows_q)
+    for ds in range(sides):
+        for dc in range(2):
+            ef_core(ds, dc, True).wait_recv()
+    rows_e = got_e[...].reshape(spare_row, width)
+    total[...] += dot(mask_e[...], rows_e)
+
+    for dg, dr in steps:
+        pair_in(rank_bufs, dg, dr).wait_recv()
+
+    def collect(ref, parts, scale):
+        upper, lower = parts(ref[...].reshape(owners, LANES))
+        both = dot(jnp.concatenate([upper, lower], axis=0), place)
+        return jnp.sum(
+            owned_f * (scale * both[0:owners] + both[owners:]), axis=0, keepdims=True
+        )
+
+    rank_ref[...] = collect(got_rank, digits, 256.0).astype(jnp.int32)
+
+    for dg, dr in steps:
+        pair_in(d_bufs, dg, dr).wait_recv()
+    rows_d = got_d[...].reshape(direct_row, width)
+    sums = total[...] + dot(mask_d[...], rows_d)
+    share = 1.0 / jnp.maximum(seen, 1.0)
+    norm = share * jnp.sqrt(jnp.sum(sums * sums, axis=1, keepdims=True))
+    cent_ref[...] = (sums * (share / jnp.maximum(norm, norm_floor))).astype(BF16)
+
+    def near(mask_ref, begin_at, end_at, block_rows):
+        score = dot_nt(cent_ref[...], block_rows)
+        return jnp.sum(
+            mask_ref[:, begin_at:end_at].astype(F32) * score, axis=0, keepdims=True
+        )
+
+    half = spare_row // 2
+    nears = jnp.concatenate([
+        near(mask_d, 0, direct_row, got_d[...].reshape(direct_row, width)),
+        near(mask_q, 0, shared_row, got_q[...].reshape(shared_row, width)),
+        near(mask_e, 0, half, got_e[0 : groups // 2].reshape(half, width)),
+        near(mask_e, half, spare_row, got_e[groups // 2 :].reshape(half, width)),
+    ], axis=1)
+    upper, lower = by_source(nears, split)
+    send_dist[...] = (upper + lower).reshape(owners, 1, LANES)
+    got_dist[me] = send_dist[me]
+    for dg, dr in steps:
+        pair_out(dist_bufs, dg, dr).start()
+
+    for bufs in (id_bufs, d_bufs, rank_bufs):
+        for dg, dr in steps:
+            pair_out(bufs, dg, dr).wait_send()
+    for dp in range(1, planes):
+        e_plane(dp, False).wait_send()
+    for dr in range(1, replicas):
+        q_out(dr).wait_send()
+    for ds, dc in others:
+        ef_side(ds, dc, False).wait_send()
+    for ds in range(1, sides):
+        qf_side(ds, False).wait_send()
+    for ds in range(sides):
+        qf_core(ds, False).wait_send()
+        for dc in range(2):
+            ef_core(ds, dc, False).wait_send()
+
+    for dg, dr in steps:
+        pair_in(dist_bufs, dg, dr).wait_recv()
+    dist_ref[...] = 1.0 - collect(got_dist, split, 1.0)
+    for dg, dr in steps:
+        pair_out(dist_bufs, dg, dr).wait_send()
+
+
 def solution(mesh):
     groups, replicas = mesh.shape["grp"], mesh.shape["rep"]
     owners = groups * replicas
@@ -289,33 +685,33 @@
         rows, width = embeddings.shape
         limit = CL_DEV + CL_DEV // 2
         most = -(-(3 * rows // owners) // 16) * 16
-        direct = -(-2 * most // 48) * 16
+        direct, shared, spare = 16, 16, 32
         vmem = pl.BlockSpec(memory_space=pltpu.VMEM)
-        small = pltpu.VMEM((owners, 8, LANES), F32)
         each = pltpu.SemaphoreType.DMA((owners,))
-        near = pltpu.SemaphoreType.DMA((replicas,))
-        far = pltpu.SemaphoreType.DMA((groups,))
-        ids_row, edges = cluster_ids.reshape(1, rows), owner_bounds.reshape(owners, 1)
-
-        def run(direct, extra, number):
-            slots = direct + extra
+        ids_row = cluster_ids.reshape(1, rows)
+        outs = (
+            jax.ShapeDtypeStruct((limit, width), BF16),
+            jax.ShapeDtypeStruct((1, rows), F32),
+            jax.ShapeDtypeStruct((1, rows), jnp.int32),
+            jax.ShapeDtypeStruct((1, LANES), jnp.int32),
+        )
+
+        def run(number):
+            small = pltpu.VMEM((owners, 8, LANES), F32)
+            near = pltpu.SemaphoreType.DMA((replicas,))
+            far = pltpu.SemaphoreType.DMA((groups,))
             return pl.pallas_call(
-                functools.partial(kernel, groups, replicas, direct, extra),
-                out_shape=(
-                    jax.ShapeDtypeStruct((limit, width), BF16),
-                    jax.ShapeDtypeStruct((1, rows), F32),
-                    jax.ShapeDtypeStruct((1, rows), jnp.int32),
-                    jax.ShapeDtypeStruct((1, LANES), jnp.int32),
-                ),
+                functools.partial(kernel, groups, replicas, most, 0),
+                out_shape=outs,
                 in_specs=[vmem] * 3,
                 out_specs=(vmem,) * 4,
                 scratch_shapes=[
                     pltpu.VMEM((rows, width), BF16),
-                    pltpu.VMEM((owners, direct, width), BF16),
-                    pltpu.VMEM((owners, slots, width), BF16),
+                    pltpu.VMEM((owners, most, width), BF16),
+                    pltpu.VMEM((owners, most, width), BF16),
                     small,
                     small,
-                    pltpu.VMEM((groups, limit, replicas * slots), BF16),
+                    pltpu.VMEM((groups, limit, replicas * most), BF16),
                     pltpu.VMEM((limit, width), F32),
                     small,
                     small,
@@ -327,15 +723,55 @@
                     has_side_effects=True,
                     vmem_limit_bytes=48 * 1024 * 1024,
                 ),
-            )(embeddings, ids_row, edges)
-
-        if direct >= most:
-            centroids, distance, rank, _ = run(most, 0, 0)
+            )(embeddings, ids_row, owner_bounds.reshape(owners, 1))
+
+        def run_fast(number):
+            small = pltpu.VMEM((owners, 1, LANES), F32)
+            slots = owners * (direct + shared + spare)
+            return pl.pallas_call(
+                functools.partial(fast_kernel, groups, replicas, direct, shared, spare),
+                out_shape=outs,
+                in_specs=[vmem] * 3,
+                out_specs=(vmem,) * 4,
+                scratch_shapes=[
+                    pltpu.VMEM((rows, width), BF16),
+                    pltpu.VMEM((owners, direct, width), BF16),
+                    pltpu.VMEM((replicas, shared, width), BF16),
+                    pltpu.VMEM((owners, direct, width), BF16),
+                    pltpu.VMEM((groups, replicas, shared, width), BF16),
+                    pltpu.VMEM((groups, 2, replicas // 2, spare, width), BF16),
+                    small, small, small, small, small, small,
+                    pltpu.VMEM((limit, owners * direct), BF16),
+                    pltpu.VMEM((limit, owners * shared), BF16),
+                    pltpu.VMEM((limit, owners * spare), BF16),
+                    pltpu.VMEM((limit, width), F32),
+                    pltpu.VMEM((1, slots), F32),
+                    pltpu.VMEM((slots, LANES), BF16),
+                    each, each, each, each, each, each, each, each,
+                    pltpu.SemaphoreType.DMA((replicas,)),
+                    pltpu.SemaphoreType.DMA((replicas,)),
+                    pltpu.SemaphoreType.DMA((groups,)),
+                    pltpu.SemaphoreType.DMA((groups,)),
+                    pltpu.SemaphoreType.DMA((replicas // 2,)),
+                    pltpu.SemaphoreType.DMA((replicas // 2,)),
+                    pltpu.SemaphoreType.DMA((2 * groups,)),
+                    pltpu.SemaphoreType.DMA((2 * groups,)),
+                ],
+                compiler_params=pltpu.CompilerParams(
+                    collective_id=number,
+                    has_side_effects=True,
+                    vmem_limit_bytes=48 * 1024 * 1024,
+                ),
+            )(embeddings, ids_row, owner_bounds.reshape(1, owners))
+
+        whole = groups % 2 == 0 and replicas * direct == LANES and rows // owners <= direct
+        if most > 2 * direct and whole:
+            first = run_fast(0)
+            centroids, distance, rank = lax.cond(
+                first[3][0, LANES - 1] > 0, lambda: run(1)[:3], lambda: first[:3]
+            )
         else:
-            first = run(direct, most - direct, 0)
-            centroids, distance, rank = lax.cond(
-                first[3][0, 0] > 0, lambda: run(most, 0, 1)[:3], lambda: first[:3]
-            )
+            centroids, distance, rank, _ = run(0)
         return distance.reshape(rows), rank.reshape(rows), centroids[None]
 
     placed = (P(("grp", "rep"), None), P(("grp", "rep")), P())

time: 68.6 us -> 54.4 us (0.79)
  Pallas kernels: 64.1 us -> 49.6 us
    pallas_call x1, Pallas kernels: 64.1 us -> 49.6 us  [run_fast(): pl.pallas_call(functools.partial(fast_kernel, groups, replicas, direct, s...]
    reshape x1 -> x0, local copies, waits for them, and re-layouts: 0.81 us -> none  [shards(): owner_bounds.reshape(owners, 1)]
where the time goes in v1:
time: 54.4 us; the launch traced here: 54.2 us
  Pallas kernels  49.6 us (91%)
  local copies, waits for them, and re-layouts  3.31 us (6%)
  between operations  1.33 us (2%)
    pallas_call x1, Pallas kernels, run_fast(): pl.pallas_call(functools.partial(fast_kernel, groups, replicas, direct, s...  49.6 us
    unnamed x9, local copies, waits for them, and re-layouts  2.73 us

profile of v1, /device:TPU:0, one launch (start us, length us, event | category | flops | bytes accessed | tf_op | source)
XLA Modules:
  0.0 54.2 jit_solution(17216733349189799165)
XLA Ops:
  0.6 0.0 copy-start
  0.6 49.6 %shard_map.58 = (bf16[576,768]{1,0:T(8,128)(2,1)S(1)}, f32[1,512]{1,0:T(1,128)S(1)}, s32[1,512]{1,0:T(1,128)S(1)}, s32[1,128]{1,0:T(1,128)S(1)}) custom-call(bf16[512,768]{1,0:T(8,128)(2,1)} %emb_ref.1, s32[1,512]{1,0:T(1,128)} %bitcast.12, s32[1,32]{1,0:T(1,128)} %bitcast.18), custom_call_target="tpu_custom_call" | custom-call | tf_op jit(solution)/shard_map/pallas_call | solution.py:731
  50.2 0.6 %slice.3 = s32[1,1]{1,0:T(1,128)} slice(s32[1,128]{1,0:T(1,128)S(1)} %get-tuple-element.46), slice={[0:1], [127:128]} | slice | bytes 8 | tf_op jit(solution)/shard_map/slice | solution.py:771
  51.5 0.0 copy-start.1
  51.5 0.0 copy-start.2
  51.5 0.0 copy-done
  51.5 0.7 %copy-done.1 = s32[512]{0:T(512)S(1)} copy-done((s32[512]{0:T(512)S(1)}, s32[512]{0:T(512)}, u32[]{:S(2)}) %copy-start.1) | copy-done | bytes 2072
  52.2 0.0 copy-done.2
  52.2 0.6 %copy.19 = f32[512]{0:T(512)} copy(f32[512]{0:T(512)S(1)} %get-tuple-element.71) | data formatting | bytes 4096
  52.8 0.6 %copy.20 = s32[512]{0:T(512)} copy(s32[512]{0:T(512)S(1)} %get-tuple-element.72) | data formatting | bytes 4096
  53.3 0.9 %copy.21 = bf16[1,576,768]{2,1,0:T(8,128)(2,1)} copy(bf16[1,576,768]{2,1,0:T(8,128)(2,1)S(1)} %get-tuple-element.73) | data formatting | bytes 1769472
  (1 shorter events, 0.0 us)
Async XLA Ops:
  0.6 50.9 %copy-start = (bf16[512,768]{1,0:T(8,128)(2,1)S(1)}, bf16[512,768]{1,0:T(8,128)(2,1)}, u32[]{:S(2)}) copy-start(bf16[512,768]{1,0:T(8,128)(2,1)} %emb_ref.1) | copy-start | bytes 2359300
  51.5 0.7 %copy-start.1 = (s32[512]{0:T(512)S(1)}, s32[512]{0:T(512)}, u32[]{:S(2)}) copy-start(s32[512]{0:T(512)} %param.6) | copy-start | bytes 6148
  51.5 0.7 %copy-start.2 = (s32[32]{0:T(128)S(1)}, s32[32]{0:T(128)}, u32[]{:S(2)}) copy-start(s32[32]{0:T(128)} %param.7) | copy-start | bytes 388

commit v2 on v1

--- a/solution.py
+++ b/solution.py
@@ -37,8 +37,9 @@
 
 def kernel(
     groups, replicas, direct, extra,
-    emb_ref, ids_ref, bounds_ref,
+    emb_in, ids_in, bounds_in,
     cent_ref, dist_ref, rank_ref, over_ref,
+    emb_ref, ids_ref, bounds_ref, in_sems,
     unit, send_rows, got_rows, send_ids, got_ids, member, total, ret, got_ret, slot_mat,
     row_send, row_recv, id_send, id_recv, ret_send, ret_recv,
     near_send, near_recv, far_send, far_recv,
@@ -106,8 +107,18 @@
             ),
         )
 
+    loads = [
+        pltpu.make_async_copy(emb_in, emb_ref, in_sems.at[0]),
+        pltpu.make_async_copy(ids_in, ids_ref, in_sems.at[1]),
+        pltpu.make_async_copy(bounds_in, bounds_ref, in_sems.at[2]),
+    ]
+    for load in loads:
+        load.start()
+    for load in loads:
+        load.wait()
     ids = ids_ref[...]
-    edges = bounds_ref[...]
+    diagonal = iota((owners, owners), 0) == iota((owners, owners), 1)
+    edges = jnp.sum(jnp.where(diagonal, bounds_ref[...], 0), axis=1, keepdims=True)
     reached = ones_at(edges <= ids, F32)
     owner = jnp.sum(reached, axis=0, keepdims=True).astype(jnp.int32) - 1
     owned = iota((owners, rows), 0) == owner
@@ -201,7 +212,7 @@
     for dg in order:
         every(dg, lambda dr, dg=dg: wait_recv(id_bufs, dg, dr))
     worst = jnp.max(got_ids[:, 1, :], axis=0, keepdims=True)
-    over_ref[...] = jnp.where(worst > extra, 1, 0)
+    over_ref[0, 0] = jnp.where(jnp.max(worst) > extra, 1, 0)
     begin = jnp.sum(
         jnp.where(iota((owners, 1), 0) == me, edges, 0), axis=0, keepdims=True
     ).astype(F32)
@@ -305,8 +316,9 @@
 
 def fast_kernel(
     groups, replicas, direct, shared, spare,
-    emb_ref, ids_ref, bounds_ref,
-    cent_ref, dist_ref, rank_ref, over_ref,
+    emb_in, ids_in, bounds_in,
+    cent_ref, dist_ref, rank_ref, over_ref, ids_ref, bounds_ref,
+    emb_ref, in_sems,
     unit, send_d, send_q, got_d, got_q, got_e,
     send_ids, got_ids, send_rank, got_rank, send_dist, got_dist,
     mask_d, mask_q, mask_e, total, ranks, spread,
@@ -425,6 +437,15 @@
         at = groups + ds * 2 + dc
         return remote(ref, ref, ef_send.at[at], ef_recv.at[at], sibling)
 
+    loads = [
+        pltpu.make_async_copy(ids_in, ids_ref, in_sems.at[0]),
+        pltpu.make_async_copy(bounds_in, bounds_ref, in_sems.at[1]),
+        pltpu.make_async_copy(emb_in, emb_ref, in_sems.at[2]),
+    ]
+    for load in loads:
+        load.start()
+    loads[0].wait()
+    loads[1].wait()
     ids = ids_ref[...]
     bounds = bounds_ref[...]
     diagonal = iota((owners, owners), 0) == iota((owners, owners), 1)
@@ -452,6 +473,7 @@
     )[0:1, :].astype(jnp.int32)
     count = jnp.sum(spare_f, axis=1, keepdims=True)
 
+    loads[2].wait()
     values = emb_ref[...].astype(F32)
     unit[...] = (
         values * lax.rsqrt(jnp.sum(values * values, axis=1, keepdims=True) + epsilon)
@@ -558,8 +580,7 @@
     for dg, dr in steps:
         pair_in(id_bufs, dg, dr).wait_recv()
     named = got_ids[...].reshape(owners, LANES)
-    worst = jnp.max(named, axis=0, keepdims=True)
-    over_ref[...] = jnp.where(worst > spare, 1, 0)
+    over_ref[0, 0] = jnp.where(jnp.max(named[:, used:]) > spare, 1, 0)
     begin = jnp.sum(jnp.where(iota((owners, 1), 0) == me, edges, 0), axis=0, keepdims=True)
     ending = jnp.sum(
         jnp.where(iota((owners, 1), 0) == me + 1, edges, 0), axis=0, keepdims=True
@@ -677,6 +698,23 @@
         pair_out(dist_bufs, dg, dr).wait_send()
 
 
+def store_kernel(cent_ref, dist_ref, rank_ref, cent_out, dist_out, rank_out, sems):
+    pieces = sems.shape[0] - 2
+    size = cent_ref.shape[0] // pieces
+    copies = [
+        pltpu.make_async_copy(
+            cent_ref.at[pl.ds(at * size, size)], cent_out.at[pl.ds(at * size, size)], sems.at[at]
+        )
+        for at in range(pieces)
+    ]
+    copies.append(pltpu.make_async_copy(dist_ref, dist_out, sems.at[pieces]))
+    copies.append(pltpu.make_async_copy(rank_ref, rank_out, sems.at[pieces + 1]))
+    for copy in copies:
+        copy.start()
+    for copy in copies:
+        copy.wait()
+
+
 def solution(mesh):
     groups, replicas = mesh.shape["grp"], mesh.shape["rep"]
     owners = groups * replicas
@@ -687,25 +725,33 @@
         most = -(-(3 * rows // owners) // 16) * 16
         direct, shared, spare = 16, 16, 32
         vmem = pl.BlockSpec(memory_space=pltpu.VMEM)
+        scalar = pl.BlockSpec(memory_space=pltpu.SMEM)
+        anywhere = pl.BlockSpec(memory_space=pl.ANY)
+        outside = pl.BlockSpec(memory_space=pltpu.HBM)
         each = pltpu.SemaphoreType.DMA((owners,))
         ids_row = cluster_ids.reshape(1, rows)
+        bounds_row = owner_bounds.reshape(1, owners)
         outs = (
             jax.ShapeDtypeStruct((limit, width), BF16),
             jax.ShapeDtypeStruct((1, rows), F32),
             jax.ShapeDtypeStruct((1, rows), jnp.int32),
-            jax.ShapeDtypeStruct((1, LANES), jnp.int32),
-        )
-
-        def run(number):
+            jax.ShapeDtypeStruct((1, 1), jnp.int32),
+        )
+
+        def run(number, ids_in, bounds_in):
             small = pltpu.VMEM((owners, 8, LANES), F32)
             near = pltpu.SemaphoreType.DMA((replicas,))
             far = pltpu.SemaphoreType.DMA((groups,))
             return pl.pallas_call(
                 functools.partial(kernel, groups, replicas, most, 0),
                 out_shape=outs,
-                in_specs=[vmem] * 3,
-                out_specs=(vmem,) * 4,
+                in_specs=[anywhere] * 3,
+                out_specs=(vmem, vmem, vmem, scalar),
                 scratch_shapes=[
+                    pltpu.VMEM((rows, width), BF16),
+                    pltpu.VMEM((1, rows), jnp.int32),
+                    pltpu.VMEM((1, owners), jnp.int32),
+                    pltpu.SemaphoreType.DMA((3,)),
                     pltpu.VMEM((rows, width), BF16),
                     pltpu.VMEM((owners, most, width), BF16),
                     pltpu.VMEM((owners, most, width), BF16),
@@ -723,17 +769,22 @@
                     has_side_effects=True,
                     vmem_limit_bytes=48 * 1024 * 1024,
                 ),
-            )(embeddings, ids_row, owner_bounds.reshape(owners, 1))
+            )(embeddings, ids_in, bounds_in)
 
         def run_fast(number):
             small = pltpu.VMEM((owners, 1, LANES), F32)
             slots = owners * (direct + shared + spare)
             return pl.pallas_call(
                 functools.partial(fast_kernel, groups, replicas, direct, shared, spare),
-                out_shape=outs,
-                in_specs=[vmem] * 3,
-                out_specs=(vmem,) * 4,
+                out_shape=outs + (
+                    jax.ShapeDtypeStruct((1, rows), jnp.int32),
+                    jax.ShapeDtypeStruct((1, owners), jnp.int32),
+                ),
+                in_specs=[outside] * 3,
+                out_specs=(vmem, vmem, vmem, scalar, vmem, vmem),
                 scratch_shapes=[
+                    pltpu.VMEM((rows, width), BF16),
+                    pltpu.SemaphoreType.DMA((3,)),
                     pltpu.VMEM((rows, width), BF16),
                     pltpu.VMEM((owners, direct, width), BF16),
                     pltpu.VMEM((replicas, shared, width), BF16),
@@ -762,16 +813,23 @@
                     has_side_effects=True,
                     vmem_limit_bytes=48 * 1024 * 1024,
                 ),
-            )(embeddings, ids_row, owner_bounds.reshape(1, owners))
+            )(*(pltpu.with_memory_space_constraint(x, pltpu.HBM) for x in (embeddings, ids_row, bounds_row)))
 
         whole = groups % 2 == 0 and replicas * direct == LANES and rows // owners <= direct
         if most > 2 * direct and whole:
             first = run_fast(0)
             centroids, distance, rank = lax.cond(
-                first[3][0, LANES - 1] > 0, lambda: run(1)[:3], lambda: first[:3]
+                first[3][0, 0] > 0, lambda: run(1, first[4], first[5])[:3], lambda: first[:3]
             )
         else:
-            centroids, distance, rank, _ = run(0)
+            centroids, distance, rank, _ = run(0, ids_row, bounds_row)
+        centroids, distance, rank = pl.pallas_call(
+            store_kernel,
+            out_shape=outs[:3],
+            in_specs=[vmem] * 3,
+            out_specs=(anywhere,) * 3,
+            scratch_shapes=[pltpu.SemaphoreType.DMA((6,))],
+        )(centroids, distance, rank)
         return distance.reshape(rows), rank.reshape(rows), centroids[None]
 
     placed = (P(("grp", "rep"), None), P(("grp", "rep")), P())

time: 54.4 us -> 52.2 us (0.960)
  local copies, waits for them, and re-layouts: 3.31 us -> 0.01 us
  Pallas kernels: 49.6 us -> 50.3 us
    unnamed x9 -> x2, local copies, waits for them, and re-layouts: 2.73 us -> 0.01 us
    pallas_call x0 -> x1, Pallas kernels: none -> 0.96 us  [shards(): pl.pallas_call(store_kernel, out_shape=outs[:3], in_specs=[vmem] * 3, out...]
    slice x1 -> x0, local copies, waits for them, and re-layouts: 0.58 us -> none  [shards(): first[3][0, LANES - 1] > 0]
where the time goes in v2:
time: 52.2 us; the launch traced here: 52 us
  Pallas kernels  50.3 us (96%)
  between operations  1.51 us (3%)
    pallas_call x1, Pallas kernels, run_fast(): pl.pallas_call(functools.partial(fast_kernel, groups, replicas, direct, s...  49.4 us

profile of v2, /device:TPU:0, one launch (start us, length us, event | category | flops | bytes accessed | tf_op | source)
XLA Modules:
  0.0 52.0 jit_solution(10263858941532525439)
XLA Ops:
  0.6 0.0 copy-start
  0.6 49.4 %shard_map.58 = (bf16[576,768]{1,0:T(8,128)(2,1)S(1)}, f32[1,512]{1,0:T(1,128)S(1)}, s32[1,512]{1,0:T(1,128)S(1)}, s32[1,1]{1,0:T(1,128)}, s32[1,512]{1,0:T(1,128)S(1)}, /*index=5*/s32[1,32]{1,0:T(1,128)S(1)}) custom-call(bf16[512,768]{1,0:T(8,128)(2,1)} %emb_in.1, s32[1,512]{1,0:T(1,128)} %bitcast.6, s32[1,32]{1,0:T(1,128)} %bitcast.7), custom_call_target="tpu_custom_call" | custom-call | tf_op jit(solution)/shard_map/pallas_call | solution.py:777
  50.7 0.0 copy-done
  50.7 0.2 conditional.1
  50.9 1.0 %shard_map.59 = (bf16[576,768]{1,0:T(8,128)(2,1)}, f32[1,512]{1,0:T(1,128)}, s32[1,512]{1,0:T(1,128)}) custom-call(bf16[576,768]{1,0:T(8,128)(2,1)S(1)} %get-tuple-element.39.cent_ref, f32[1,512]{1,0:T(1,128)S(1)} %get-tuple-element.40.dist_ref, s32[1,512]{1,0:T(1,128)S(1)} %get-tuple-element.41.rank_ref), custom_call_target="tpu_custom_call" | custom-call | tf_op jit(solution)/shard_map/pallas_call | solution.py:826
Async XLA Ops:
  0.6 50.1 %copy-start = (bf16[512,768]{1,0:T(8,128)(2,1)S(1)}, bf16[512,768]{1,0:T(8,128)(2,1)}, u32[]{:S(2)}) copy-start(bf16[512,768]{1,0:T(8,128)(2,1)} %emb_in.1) | copy-start | bytes 2359300

commit v3 on v2

--- a/solution.py
+++ b/solution.py
@@ -422,12 +422,20 @@
         col = lax.rem(my_col + dc, 2)
         return side * 2 + my_core, col
 
-    def ef_side(ds, dc, inward):
-        group, col = e_spot(ds, dc, inward)
-        ref = got_e.at[group, col] if inward else got_e.at[my_group, my_col]
-        at = ds * 2 + dc
+    def ef_side(ds, inward):
+        group = e_spot(ds, 0, inward)[0]
+        ref = got_e.at[group if inward else my_group, my_col]
         return remote(
-            ref, ref, ef_send.at[at], ef_recv.at[at], (group, my_plane * 2 + col)
+            ref, ref, ef_send.at[2 * ds], ef_recv.at[2 * ds], (group, my_replica)
+        )
+
+    def ef_col(ds, inward):
+        group = e_spot(ds, 0, True)[0]
+        ref = got_e.at[group, 1 - my_col if inward else my_col]
+        at = 2 * ds + 1
+        return remote(
+            ref, ref, ef_send.at[at], ef_recv.at[at],
+            (my_group, my_plane * 2 + (1 - my_col)),
         )
 
     def ef_core(ds, dc, inward):
@@ -525,15 +533,28 @@
 
     for dp in range(1, planes):
         e_plane(dp, True).wait_recv()
-    others = [(ds, dc) for ds in range(sides) for dc in range(2) if ds or dc]
-    for ds, dc in others:
-        ef_side(ds, dc, False).start()
+    for ds in range(1, sides):
+        ef_side(ds, False).start()
+    ef_col(0, False).start()
     ef_core(0, 0, False).start()
     for dr in range(1, replicas):
         q_in(dr).wait_recv()
     for ds in range(1, sides):
         qf_side(ds, False).start()
     qf_core(0, False).start()
+
+    def forward_sides():
+        for ds in range(1, sides):
+            ef_side(ds, True).wait_recv()
+            ef_col(ds, False).start()
+            ef_core(ds, 0, False).start()
+        for ds in range(1, sides):
+            qf_side(ds, True).wait_recv()
+            qf_core(ds, False).start()
+
+    def forward_col(ds):
+        ef_col(ds, True).wait_recv()
+        ef_core(ds, 1, False).start()
 
     direct_row, shared_row, spare_row = groups * block, owners * shared, owners * spare
     d_lane, q_lane, e_lane = fold(block, direct), fold(block, shared), fold(replicas * spare, spare)
@@ -612,6 +633,8 @@
         at = direct_row + shared_row + sg * wide
         ranks[:, at : at + wide] = slot[:, 2 * block :]
         seen = seen + jnp.sum(mask, axis=1, keepdims=True)
+        if sg == 1:
+            forward_sides()
 
     upper, lower = by_source(ranks[...], digits)
     send_rank[...] = (256.0 * upper + lower).reshape(owners, 1, LANES)
@@ -619,12 +642,8 @@
     for dg, dr in steps:
         pair_out(rank_bufs, dg, dr).start()
 
-    for ds in range(1, sides):
-        qf_side(ds, True).wait_recv()
-        qf_core(ds, False).start()
-    for ds, dc in others:
-        ef_side(ds, dc, True).wait_recv()
-        ef_core(ds, dc, False).start()
+    for ds in range(sides):
+        forward_col(ds)
 
     for ds in range(sides):
         qf_core(ds, True).wait_recv()
@@ -636,8 +655,6 @@
     rows_e = got_e[...].reshape(spare_row, width)
     total[...] += dot(mask_e[...], rows_e)
 
-    for dg, dr in steps:
-        pair_in(rank_bufs, dg, dr).wait_recv()
 
     def collect(ref, parts, scale):
         upper, lower = parts(ref[...].reshape(owners, LANES))
@@ -646,7 +663,6 @@
             owned_f * (scale * both[0:owners] + both[owners:]), axis=0, keepdims=True
         )
 
-    rank_ref[...] = collect(got_rank, digits, 256.0).astype(jnp.int32)
 
     for dg, dr in steps:
         pair_in(d_bufs, dg, dr).wait_recv()
@@ -675,6 +691,9 @@
     for dg, dr in steps:
         pair_out(dist_bufs, dg, dr).start()
 
+    for dg, dr in steps:
+        pair_in(rank_bufs, dg, dr).wait_recv()
+    rank_ref[...] = collect(got_rank, digits, 256.0).astype(jnp.int32)
     for bufs in (id_bufs, d_bufs, rank_bufs):
         for dg, dr in steps:
             pair_out(bufs, dg, dr).wait_send()
@@ -682,12 +701,13 @@
         e_plane(dp, False).wait_send()
     for dr in range(1, replicas):
         q_out(dr).wait_send()
-    for ds, dc in others:
-        ef_side(ds, dc, False).wait_send()
+    for ds in range(1, sides):
+        ef_side(ds, False).wait_send()
     for ds in range(1, sides):
         qf_side(ds, False).wait_send()
     for ds in range(sides):
         qf_core(ds, False).wait_send()
+        ef_col(ds, False).wait_send()
         for dc in range(2):
             ef_core(ds, dc, False).wait_send()
 

time: 52.2 us -> 49.4 us (0.946)
  Pallas kernels: 50.3 us -> 47.5 us
    pallas_call x1, Pallas kernels: 49.4 us -> 46.6 us  [run_fast(): pl.pallas_call(functools.partial(fast_kernel, groups, replicas, direct, s...]
where the time goes in v3:
time: 49.4 us; the launch traced here: 49.2 us
  Pallas kernels  47.5 us (96%)
  between operations  1.51 us (3%)
    pallas_call x1, Pallas kernels, run_fast(): pl.pallas_call(functools.partial(fast_kernel, groups, replicas, direct, s...  46.6 us

profile of v3, /device:TPU:0, one launch (start us, length us, event | category | flops | bytes accessed | tf_op | source)
XLA Modules:
  0.0 49.2 jit_solution(13903424585040983911)
XLA Ops:
  0.6 0.0 copy-start
  0.6 46.6 %shard_map.58 = (bf16[576,768]{1,0:T(8,128)(2,1)S(1)}, f32[1,512]{1,0:T(1,128)S(1)}, s32[1,512]{1,0:T(1,128)S(1)}, s32[1,1]{1,0:T(1,128)}, s32[1,512]{1,0:T(1,128)S(1)}, /*index=5*/s32[1,32]{1,0:T(1,128)S(1)}) custom-call(bf16[512,768]{1,0:T(8,128)(2,1)} %emb_in.1, s32[1,512]{1,0:T(1,128)} %bitcast.6, s32[1,32]{1,0:T(1,128)} %bitcast.7), custom_call_target="tpu_custom_call" | custom-call | tf_op jit(solution)/shard_map/pallas_call | solution.py:797
  47.9 0.0 copy-done
  47.9 0.2 conditional.1
  48.1 1.0 %shard_map.59 = (bf16[576,768]{1,0:T(8,128)(2,1)}, f32[1,512]{1,0:T(1,128)}, s32[1,512]{1,0:T(1,128)}) custom-call(bf16[576,768]{1,0:T(8,128)(2,1)S(1)} %get-tuple-element.39.cent_ref, f32[1,512]{1,0:T(1,128)S(1)} %get-tuple-element.40.dist_ref, s32[1,512]{1,0:T(1,128)S(1)} %get-tuple-element.41.rank_ref), custom_call_target="tpu_custom_call" | custom-call | tf_op jit(solution)/shard_map/pallas_call | solution.py:846
Async XLA Ops:
  0.6 47.3 %copy-start = (bf16[512,768]{1,0:T(8,128)(2,1)S(1)}, bf16[512,768]{1,0:T(8,128)(2,1)}, u32[]{:S(2)}) copy-start(bf16[512,768]{1,0:T(8,128)(2,1)} %emb_in.1) | copy-start | bytes 2359300

commit v4 on v3

--- a/solution.py
+++ b/solution.py
@@ -318,7 +318,7 @@
     groups, replicas, direct, shared, spare,
     emb_in, ids_in, bounds_in,
     cent_ref, dist_ref, rank_ref, over_ref, ids_ref, bounds_ref,
-    emb_ref, in_sems,
+    emb_ref, in_sems, over,
     unit, send_d, send_q, got_d, got_q, got_e,
     send_ids, got_ids, send_rank, got_rank, send_dist, got_dist,
     mask_d, mask_q, mask_e, total, ranks, spread,
@@ -377,6 +377,16 @@
     id_bufs = (send_ids, got_ids, id_send, id_recv)
     rank_bufs = (send_rank, got_rank, rank_send, rank_recv)
     dist_bufs = (send_dist, got_dist, dist_send, dist_recv)
+
+    low, half = lax.rem(my_plane, 2), lax.div(my_plane, 2)
+    plane_order = [
+        my_plane, half * 2 + (1 - low), (1 - half) * 2 + low, (1 - half) * 2 + (1 - low)
+    ]
+
+    def d_out(plane, dg, dc):
+        pair = (to_group[dg], plane * 2 + lax.rem(my_col + dc, 2))
+        there = pair[0] * replicas + pair[1]
+        return remote(send_d.at[there], got_d.at[me], d_send.at[there], d_recv.at[me], pair)
 
     def q_out(dr):
         there = to_replica[dr]
@@ -512,6 +522,13 @@
     send_ids[...] = table.reshape(owners, 1, LANES)
     got_ids[me] = send_ids[me]
 
+    target = jnp.where(in_direct, owner * direct + rank, -1)
+    block = replicas * direct
+    for tg in range(groups):
+        packed = picked(block, target - tg * block)
+        send_d[tg * replicas : (tg + 1) * replicas] = packed.reshape(replicas, direct, width)
+    got_d[me] = send_d[me]
+
     pl.semaphore_wait(barrier, owners - 1)
     for dp in range(1, planes):
         e_plane(dp, False).start()
@@ -520,16 +537,11 @@
     for dg, dr in steps:
         pair_out(id_bufs, dg, dr).start()
 
-    target = jnp.where(in_direct, owner * direct + rank, -1)
-    block = replicas * direct
-    for dg in list(range(1, groups)) + [0]:
-        tg = to_group[dg]
-        packed = picked(block, target - tg * block)
-        send_d[pl.ds(tg * replicas, replicas)] = packed.reshape(replicas, direct, width)
-        for dr in range(replicas):
-            if dg or dr:
-                pair_out(d_bufs, dg, dr).start()
-    got_d[me] = send_d[me]
+    for plane in plane_order:
+        for dg in range(groups):
+            for dc in range(2):
+                if dg or dc or plane is not my_plane:
+                    d_out(plane, dg, dc).start()
 
     for dp in range(1, planes):
         e_plane(dp, True).wait_recv()
@@ -601,7 +613,9 @@
     for dg, dr in steps:
         pair_in(id_bufs, dg, dr).wait_recv()
     named = got_ids[...].reshape(owners, LANES)
-    over_ref[0, 0] = jnp.where(jnp.max(named[:, used:]) > spare, 1, 0)
+    over[0, 0] = jnp.where(jnp.max(named[:, used:]) > spare, 1, 0)
+    flag = pltpu.make_async_copy(over, over_ref, in_sems.at[3])
+    flag.start()
     begin = jnp.sum(jnp.where(iota((owners, 1), 0) == me, edges, 0), axis=0, keepdims=True)
     ending = jnp.sum(
         jnp.where(iota((owners, 1), 0) == me + 1, edges, 0), axis=0, keepdims=True
@@ -713,6 +727,7 @@
 
     for dg, dr in steps:
         pair_in(dist_bufs, dg, dr).wait_recv()
+    flag.wait()
     dist_ref[...] = 1.0 - collect(got_dist, split, 1.0)
     for dg, dr in steps:
         pair_out(dist_bufs, dg, dr).wait_send()
@@ -801,10 +816,11 @@
                     jax.ShapeDtypeStruct((1, owners), jnp.int32),
                 ),
                 in_specs=[outside] * 3,
-                out_specs=(vmem, vmem, vmem, scalar, vmem, vmem),
+                out_specs=(vmem, vmem, vmem, outside, vmem, vmem),
                 scratch_shapes=[
                     pltpu.VMEM((rows, width), BF16),
-                    pltpu.SemaphoreType.DMA((3,)),
+                    pltpu.SemaphoreType.DMA((4,)),
+                    pltpu.SMEM((1, 1), jnp.int32),
                     pltpu.VMEM((rows, width), BF16),
                     pltpu.VMEM((owners, direct, width), BF16),
                     pltpu.VMEM((replicas, shared, width), BF16),
@@ -835,21 +851,27 @@
                 ),
             )(*(pltpu.with_memory_space_constraint(x, pltpu.HBM) for x in (embeddings, ids_row, bounds_row)))
 
-        whole = groups % 2 == 0 and replicas * direct == LANES and rows // owners <= direct
+        def stored(results):
+            return tuple(
+                pl.pallas_call(
+                    store_kernel,
+                    out_shape=outs[:3],
+                    in_specs=[vmem] * 3,
+                    out_specs=(anywhere,) * 3,
+                    scratch_shapes=[pltpu.SemaphoreType.DMA((6,))],
+                    compiler_params=pltpu.CompilerParams(vmem_limit_bytes=4 * 1024 * 1024),
+                )(*results[:3])
+            )
+
+        whole = groups == 4 and replicas * direct == LANES and rows // owners <= direct
         if most > 2 * direct and whole:
             first = run_fast(0)
+            kept = stored(first)
             centroids, distance, rank = lax.cond(
-                first[3][0, 0] > 0, lambda: run(1, first[4], first[5])[:3], lambda: first[:3]
+                first[3][0, 0] > 0, lambda: stored(run(1, first[4], first[5])), lambda: kept
             )
         else:
             centroids, distance, rank, _ = run(0, ids_row, bounds_row)
-        centroids, distance, rank = pl.pallas_call(
-            store_kernel,
-            out_shape=outs[:3],
-            in_specs=[vmem] * 3,
-            out_specs=(anywhere,) * 3,
-            scratch_shapes=[pltpu.SemaphoreType.DMA((6,))],
-        )(centroids, distance, rank)
         return distance.reshape(rows), rank.reshape(rows), centroids[None]
 
     placed = (P(("grp", "rep"), None), P(("grp", "rep")), P())

time: 49.4 us -> 48.1 us (0.974)
  Pallas kernels: 47.5 us -> 46.4 us
    pallas_call x1, Pallas kernels: 46.6 us -> 45.4 us  [run_fast(): pl.pallas_call(functools.partial(fast_kernel, groups, replicas, direct, s...]
where the time goes in v4:
time: 48.1 us; the launch traced here: 48 us
  Pallas kernels  46.4 us (96%)
  between operations  1.38 us (3%)
    pallas_call x1, Pallas kernels, run_fast(): pl.pallas_call(functools.partial(fast_kernel, groups, replicas, direct, s...  45.4 us
    pallas_call x1, Pallas kernels, stored(): pl.pallas_call(store_kernel, out_shape=outs[:3], in_specs=[vmem] * 3, out...  0.96 us

profile of v4, /device:TPU:0, one launch (start us, length us, event | category | flops | bytes accessed | tf_op | source)
XLA Modules:
  0.0 48.0 jit_solution(1388032955655873149)
XLA Ops:
  0.6 0.0 copy-start
  0.6 45.4 %shard_map.58 = (bf16[576,768]{1,0:T(8,128)(2,1)S(1)}, f32[1,512]{1,0:T(1,128)S(1)}, s32[1,512]{1,0:T(1,128)S(1)}, s32[1,1]{1,0:T(1,128)}, s32[1,512]{1,0:T(1,128)S(1)}, /*index=5*/s32[1,32]{1,0:T(1,128)S(1)}) custom-call(bf16[512,768]{1,0:T(8,128)(2,1)} %emb_in.1, s32[1,512]{1,0:T(1,128)} %bitcast.9, s32[1,32]{1,0:T(1,128)} %bitcast.10), custom_call_target="tpu_custom_call" | custom-call | tf_op jit(solution)/shard_map/pallas_call | solution.py:812
  46.6 1.0 %shard_map.59 = (bf16[576,768]{1,0:T(8,128)(2,1)}, f32[1,512]{1,0:T(1,128)}, s32[1,512]{1,0:T(1,128)}) custom-call(bf16[576,768]{1,0:T(8,128)(2,1)S(1)} %get-tuple-element.55.cent_ref, f32[1,512]{1,0:T(1,128)S(1)} %get-tuple-element.56.dist_ref, s32[1,512]{1,0:T(1,128)S(1)} %get-tuple-element.57.rank_ref), custom_call_target="tpu_custom_call" | custom-call | tf_op jit(solution)/shard_map/pallas_call | solution.py:856
  47.6 0.0 copy-done
  47.6 0.2 conditional.1
Async XLA Ops:
  0.6 47.0 %copy-start = (bf16[512,768]{1,0:T(8,128)(2,1)S(1)}, bf16[512,768]{1,0:T(8,128)(2,1)}, u32[]{:S(2)}) copy-start(bf16[512,768]{1,0:T(8,128)(2,1)} %emb_in.1) | copy-start | bytes 2359300

commit v5 on v4

--- a/solution.py
+++ b/solution.py
@@ -321,7 +321,7 @@
     emb_ref, in_sems, over,
     unit, send_d, send_q, got_d, got_q, got_e,
     send_ids, got_ids, send_rank, got_rank, send_dist, got_dist,
-    mask_d, mask_q, mask_e, total, ranks, spread,
+    masks, total, ranks, spread,
     d_send, d_recv, id_send, id_recv, rank_send, rank_recv, dist_send, dist_recv,
     q_send, q_recv, qf_send, qf_recv, e_send, e_recv, ef_send, ef_recv,
 ):
@@ -373,20 +373,55 @@
         there = pair[0] * replicas + pair[1]
         return remote(src.at[there], dst.at[there], ssem.at[there], rsem.at[there], pair)
 
-    d_bufs = (send_d, got_d, d_send, d_recv)
     id_bufs = (send_ids, got_ids, id_send, id_recv)
     rank_bufs = (send_rank, got_rank, rank_send, rank_recv)
-    dist_bufs = (send_dist, got_dist, dist_send, dist_recv)
 
     low, half = lax.rem(my_plane, 2), lax.div(my_plane, 2)
     plane_order = [
         my_plane, half * 2 + (1 - low), (1 - half) * 2 + low, (1 - half) * 2 + (1 - low)
     ]
 
+    def at_plane(plane, dg, dc):
+        return to_group[dg], plane * 2 + lax.rem(my_col + dc, 2)
+
     def d_out(plane, dg, dc):
-        pair = (to_group[dg], plane * 2 + lax.rem(my_col + dc, 2))
+        pair = at_plane(plane, dg, dc)
         there = pair[0] * replicas + pair[1]
-        return remote(send_d.at[there], got_d.at[me], d_send.at[there], d_recv.at[me], pair)
+        return remote(
+            send_d.at[there], got_d.at[my_group, my_replica],
+            d_send.at[there], d_recv.at[me], pair,
+        )
+
+    def d_in(dg, dr):
+        pair = (from_group[dg], from_replica[dr])
+        there = pair[0] * replicas + pair[1]
+        return remote(
+            send_d.at[there], got_d.at[pair], d_send.at[there], d_recv.at[there], pair
+        )
+
+    def dist_out(part, plane, dg, dc):
+        pair = at_plane(plane, dg, dc)
+        there = pair[0] * replicas + pair[1]
+        return remote(
+            send_dist.at[part, there], got_dist.at[me],
+            dist_send.at[there], dist_recv.at[me], pair,
+        )
+
+    def dist_in(dg, dr):
+        pair = (from_group[dg], from_replica[dr])
+        there = pair[0] * replicas + pair[1]
+        return remote(
+            send_dist.at[0, there], got_dist.at[there],
+            dist_send.at[there], dist_recv.at[there], pair,
+        )
+
+    spots = [
+        (plane, dg, dc)
+        for plane in plane_order
+        for dg in range(groups)
+        for dc in range(2)
+        if dg or dc or plane is not my_plane
+    ]
 
     def q_out(dr):
         there = to_replica[dr]
@@ -527,7 +562,7 @@
     for tg in range(groups):
         packed = picked(block, target - tg * block)
         send_d[tg * replicas : (tg + 1) * replicas] = packed.reshape(replicas, direct, width)
-    got_d[me] = send_d[me]
+    got_d[my_group, my_replica] = send_d[me]
 
     pl.semaphore_wait(barrier, owners - 1)
     for dp in range(1, planes):
@@ -537,11 +572,8 @@
     for dg, dr in steps:
         pair_out(id_bufs, dg, dr).start()
 
-    for plane in plane_order:
-        for dg in range(groups):
-            for dc in range(2):
-                if dg or dc or plane is not my_plane:
-                    d_out(plane, dg, dc).start()
+    for spot in spots:
+        d_out(*spot).start()
 
     for dp in range(1, planes):
         e_plane(dp, True).wait_recv()
@@ -627,6 +659,46 @@
     flat_both = dot(jnp.concatenate([local_high, local_low], axis=0), expand)
     flat_all = 256.0 * flat_both[0:owners] + flat_both[owners:] - 1.0
 
+    each, width_h = replicas // 2, planes // 2
+    half_d, half_q, half_e = direct_row // 2, shared_row // 2, spare_row // 2
+    hd, hq, he = fold(half_d, direct), fold(half_q, shared), fold(half_e, spare)
+    gd, gq = fold(half_d, direct * each), fold(half_q, shared * each)
+    ge = fold(half_e, spare * each)
+    xe = fold(half_e, spare * width_h)
+    base_source = jnp.concatenate([
+        gd * replicas + hd - gd * each,
+        gq * replicas + hq - gq * each,
+        ge * replicas + (he - xe * width_h) * 2 + xe - ge * 2,
+    ], axis=1)
+    half_slot = jnp.concatenate([
+        iota((1, half_d), 1) - hd * direct,
+        iota((1, half_q), 1) - hq * shared + direct,
+        iota((1, half_e), 1) - he * spare + (direct + shared),
+    ], axis=1)
+    part_span = half_d + half_q + half_e
+    half_expand = ones_at(iota((LANES, part_span), 0) == half_slot, BF16)
+    half_both = dot(jnp.concatenate([local_high, local_low], axis=0), half_expand)
+    half_flat = 256.0 * half_both[0:owners] + half_both[owners:] - 1.0
+    part_half = [1 - half, half]
+    part_source = [base_source + at * each for at in part_half]
+    for part in range(2):
+        chosen_source = iota((owners, part_span), 0) == part_source[part]
+        flat = jnp.sum(jnp.where(chosen_source, half_flat, 0.0), axis=0, keepdims=True)
+        masks[part] = ones_at(iota((limit, part_span), 0) == flat.astype(jnp.int32), BF16)
+
+    def part_d(part):
+        return got_d[:, pl.ds(part_half[part] * each, each)].reshape(half_d, width)
+
+    def part_q(part):
+        return got_q[:, pl.ds(part_half[part] * each, each)].reshape(half_q, width)
+
+    def part_e(part):
+        return got_e[:, :, pl.ds(part_half[part] * width_h, width_h)].reshape(half_e, width)
+
+    in_d = slice(0, half_d)
+    in_q = slice(half_d, half_d + half_q)
+    in_e = slice(half_d + half_q, part_span)
+
     seen = jnp.zeros((limit, 1), F32)
     cluster = iota((limit, span), 0)
     wide = replicas * spare
@@ -636,9 +708,6 @@
         )
         mask = ones_at(cluster == flat.astype(jnp.int32), F32)
         mask_b = mask.astype(BF16)
-        mask_d[:, sg * block : (sg + 1) * block] = mask_b[:, 0:block]
-        mask_q[:, sg * block : (sg + 1) * block] = mask_b[:, block : 2 * block]
-        mask_e[:, sg * wide : (sg + 1) * wide] = mask_b[:, 2 * block :]
         ahead = dot(mask_b, before) + seen
         slot = jnp.sum(mask * ahead, axis=0, keepdims=True)
         ranks[:, sg * block : (sg + 1) * block] = slot[:, 0:block]
@@ -661,13 +730,12 @@
 
     for ds in range(sides):
         qf_core(ds, True).wait_recv()
-    rows_q = got_q[...].reshape(shared_row, width)
-    total[...] = dot(mask_q[...], rows_q)
+    total[...] = dot(masks[0, :, in_q], part_q(0)) + dot(masks[1, :, in_q], part_q(1))
     for ds in range(sides):
         for dc in range(2):
             ef_core(ds, dc, True).wait_recv()
-    rows_e = got_e[...].reshape(spare_row, width)
-    total[...] += dot(mask_e[...], rows_e)
+    for part in range(2):
+        total[...] += dot(masks[part, :, in_e], part_e(part))
 
 
     def collect(ref, parts, scale):
@@ -679,38 +747,46 @@
 
 
     for dg, dr in steps:
-        pair_in(d_bufs, dg, dr).wait_recv()
-    rows_d = got_d[...].reshape(direct_row, width)
-    sums = total[...] + dot(mask_d[...], rows_d)
+        d_in(dg, dr).wait_recv()
+    sums = total[...] + dot(masks[0, :, in_d], part_d(0)) + dot(masks[1, :, in_d], part_d(1))
     share = 1.0 / jnp.maximum(seen, 1.0)
     norm = share * jnp.sqrt(jnp.sum(sums * sums, axis=1, keepdims=True))
     cent_ref[...] = (sums * (share / jnp.maximum(norm, norm_floor))).astype(BF16)
 
-    def near(mask_ref, begin_at, end_at, block_rows):
+    def near(part, inside, block_rows):
         score = dot_nt(cent_ref[...], block_rows)
         return jnp.sum(
-            mask_ref[:, begin_at:end_at].astype(F32) * score, axis=0, keepdims=True
-        )
-
-    half = spare_row // 2
-    nears = jnp.concatenate([
-        near(mask_d, 0, direct_row, got_d[...].reshape(direct_row, width)),
-        near(mask_q, 0, shared_row, got_q[...].reshape(shared_row, width)),
-        near(mask_e, 0, half, got_e[0 : groups // 2].reshape(half, width)),
-        near(mask_e, half, spare_row, got_e[groups // 2 :].reshape(half, width)),
-    ], axis=1)
-    upper, lower = by_source(nears, split)
-    send_dist[...] = (upper + lower).reshape(owners, 1, LANES)
-    got_dist[me] = send_dist[me]
-    for dg, dr in steps:
-        pair_out(dist_bufs, dg, dr).start()
+            masks[part, :, inside].astype(F32) * score, axis=0, keepdims=True
+        )
+
+    half_spread = jnp.concatenate([
+        spread[0:half_d],
+        spread[direct_row : direct_row + half_q],
+        spread[direct_row + shared_row : direct_row + shared_row + half_e],
+    ], axis=0)
+    for part in range(2):
+        nears = jnp.concatenate([
+            near(part, in_d, part_d(part)),
+            near(part, in_q, part_q(part)),
+            near(part, in_e, part_e(part)),
+        ], axis=1)
+        held = jnp.where(iota((owners, part_span), 0) == part_source[part], nears, 0.0)
+        upper, lower = split(held)
+        both = dot(jnp.concatenate([upper, lower], axis=0), half_spread)
+        send_dist[part] = (both[0:owners] + both[owners:]).reshape(owners, 1, LANES)
+        for at, spot in enumerate(spots):
+            if (at < len(spots) - 4 * groups) == (part == 1):
+                dist_out(part, *spot).start()
+    got_dist[me] = send_dist[1, me]
 
     for dg, dr in steps:
         pair_in(rank_bufs, dg, dr).wait_recv()
     rank_ref[...] = collect(got_rank, digits, 256.0).astype(jnp.int32)
-    for bufs in (id_bufs, d_bufs, rank_bufs):
+    for bufs in (id_bufs, rank_bufs):
         for dg, dr in steps:
             pair_out(bufs, dg, dr).wait_send()
+    for spot in spots:
+        d_out(*spot).wait_send()
     for dp in range(1, planes):
         e_plane(dp, False).wait_send()
     for dr in range(1, replicas):
@@ -726,11 +802,11 @@
             ef_core(ds, dc, False).wait_send()
 
     for dg, dr in steps:
-        pair_in(dist_bufs, dg, dr).wait_recv()
+        dist_in(dg, dr).wait_recv()
     flag.wait()
     dist_ref[...] = 1.0 - collect(got_dist, split, 1.0)
-    for dg, dr in steps:
-        pair_out(dist_bufs, dg, dr).wait_send()
+    for at, spot in enumerate(spots):
+        dist_out(1 if at < len(spots) - 4 * groups else 0, *spot).wait_send()
 
 
 def store_kernel(cent_ref, dist_ref, rank_ref, cent_out, dist_out, rank_out, sems):
@@ -824,13 +900,12 @@
                     pltpu.VMEM((rows, width), BF16),
                     pltpu.VMEM((owners, direct, width), BF16),
                     pltpu.VMEM((replicas, shared, width), BF16),
-                    pltpu.VMEM((owners, direct, width), BF16),
+                    pltpu.VMEM((groups, replicas, direct, width), BF16),
                     pltpu.VMEM((groups, replicas, shared, width), BF16),
                     pltpu.VMEM((groups, 2, replicas // 2, spare, width), BF16),
-                    small, small, small, small, small, small,
-                    pltpu.VMEM((limit, owners * direct), BF16),
-                    pltpu.VMEM((limit, owners * shared), BF16),
-                    pltpu.VMEM((limit, owners * spare), BF16),
+                    small, small, small, small,
+                    pltpu.VMEM((2, owners, 1, LANES), F32), small,
+                    pltpu.VMEM((2, limit, slots // 2), BF16),
                     pltpu.VMEM((limit, width), F32),
                     pltpu.VMEM((1, slots), F32),
                     pltpu.VMEM((slots, LANES), BF16),

time: 48.1 us -> 47.6 us (0.990)
  Pallas kernels: 46.4 us -> 45.8 us
    pallas_call x1, Pallas kernels: 45.4 us -> 44.9 us  [run_fast(): pl.pallas_call(functools.partial(fast_kernel, groups, replicas, direct, s...]
where the time goes in v5:
time: 47.6 us; the launch traced here: 47.4 us
  Pallas kernels  45.8 us (96%)
  between operations  1.38 us (3%)
    pallas_call x1, Pallas kernels, run_fast(): pl.pallas_call(functools.partial(fast_kernel, groups, replicas, direct, s...  44.9 us
    pallas_call x1, Pallas kernels, stored(): pl.pallas_call(store_kernel, out_shape=outs[:3], in_specs=[vmem] * 3, out...  0.96 us

profile of v5, /device:TPU:0, one launch (start us, length us, event | category | flops | bytes accessed | tf_op | source)
XLA Modules:
  0.0 47.4 jit_solution(4964236725816015)
XLA Ops:
  0.6 0.0 copy-start
  0.6 44.9 %shard_map.58 = (bf16[576,768]{1,0:T(8,128)(2,1)S(1)}, f32[1,512]{1,0:T(1,128)S(1)}, s32[1,512]{1,0:T(1,128)S(1)}, s32[1,1]{1,0:T(1,128)}, s32[1,512]{1,0:T(1,128)S(1)}, /*index=5*/s32[1,32]{1,0:T(1,128)S(1)}) custom-call(bf16[512,768]{1,0:T(8,128)(2,1)} %emb_in.1, s32[1,512]{1,0:T(1,128)} %bitcast.9, s32[1,32]{1,0:T(1,128)} %bitcast.10), custom_call_target="tpu_custom_call" | custom-call | tf_op jit(solution)/shard_map/pallas_call | solution.py:888
  46.1 1.0 %shard_map.59 = (bf16[576,768]{1,0:T(8,128)(2,1)}, f32[1,512]{1,0:T(1,128)}, s32[1,512]{1,0:T(1,128)}) custom-call(bf16[576,768]{1,0:T(8,128)(2,1)S(1)} %get-tuple-element.55.cent_ref, f32[1,512]{1,0:T(1,128)S(1)} %get-tuple-element.56.dist_ref, s32[1,512]{1,0:T(1,128)S(1)} %get-tuple-element.57.rank_ref), custom_call_target="tpu_custom_call" | custom-call | tf_op jit(solution)/shard_map/pallas_call | solution.py:931
  47.1 0.0 copy-done
  47.1 0.2 conditional.1
Async XLA Ops:
  0.6 46.4 %copy-start = (bf16[512,768]{1,0:T(8,128)(2,1)S(1)}, bf16[512,768]{1,0:T(8,128)(2,1)}, u32[]{:S(2)}) copy-start(bf16[512,768]{1,0:T(8,128)(2,1)} %emb_in.1) | copy-start | bytes 2359300

commit v6 on v5

--- a/solution.py
+++ b/solution.py
@@ -350,7 +350,9 @@
     ]
 
     barrier = pltpu.get_barrier_semaphore()
-    for dg, dr in steps:
+    far_first = sorted(range(replicas), key=lambda dr: -min(dr, replicas - dr))
+    greeted = [(dg, dr) for dr in far_first for dg in reversed(range(groups)) if dg or dr]
+    for dg, dr in greeted:
         pl.semaphore_signal(
             barrier, inc=1, device_id=(to_group[dg], to_replica[dr]), device_id_type=MESH
         )
@@ -392,8 +394,8 @@
             d_send.at[there], d_recv.at[me], pair,
         )
 
-    def d_in(dg, dr):
-        pair = (from_group[dg], from_replica[dr])
+    def d_in(plane, dg, dc):
+        pair = at_plane(plane, dg, dc)
         there = pair[0] * replicas + pair[1]
         return remote(
             send_d.at[there], got_d.at[pair], d_send.at[there], d_recv.at[there], pair
@@ -746,9 +748,13 @@
         )
 
 
-    for dg, dr in steps:
-        d_in(dg, dr).wait_recv()
-    sums = total[...] + dot(masks[0, :, in_d], part_d(0)) + dot(masks[1, :, in_d], part_d(1))
+    close = len(spots) - 4 * groups
+    for spot in spots[:close]:
+        d_in(*spot).wait_recv()
+    total[...] += dot(masks[1, :, in_d], part_d(1))
+    for spot in spots[close:]:
+        d_in(*spot).wait_recv()
+    sums = total[...] + dot(masks[0, :, in_d], part_d(0))
     share = 1.0 / jnp.maximum(seen, 1.0)
     norm = share * jnp.sqrt(jnp.sum(sums * sums, axis=1, keepdims=True))
     cent_ref[...] = (sums * (share / jnp.maximum(norm, norm_floor))).astype(BF16)
@@ -774,9 +780,8 @@
         upper, lower = split(held)
         both = dot(jnp.concatenate([upper, lower], axis=0), half_spread)
         send_dist[part] = (both[0:owners] + both[owners:]).reshape(owners, 1, LANES)
-        for at, spot in enumerate(spots):
-            if (at < len(spots) - 4 * groups) == (part == 1):
-                dist_out(part, *spot).start()
+        for spot in (spots[:close] if part else spots[close:])[::-1]:
+            dist_out(part, *spot).start()
     got_dist[me] = send_dist[1, me]
 
     for dg, dr in steps:

time: 47.6 us -> 47 us (0.987)
  Pallas kernels: 45.8 us -> 45.3 us
    pallas_call x1, Pallas kernels: 44.9 us -> 44.3 us  [run_fast(): pl.pallas_call(functools.partial(fast_kernel, groups, replicas, direct, s...]
where the time goes in v6:
time: 47 us; the launch traced here: 46.8 us
  Pallas kernels  45.3 us (96%)
  between operations  1.38 us (3%)
    pallas_call x1, Pallas kernels, run_fast(): pl.pallas_call(functools.partial(fast_kernel, groups, replicas, direct, s...  44.3 us
    pallas_call x1, Pallas kernels, stored(): pl.pallas_call(store_kernel, out_shape=outs[:3], in_specs=[vmem] * 3, out...  0.96 us

profile of v6, /device:TPU:0, one launch (start us, length us, event | category | flops | bytes accessed | tf_op | source)
XLA Modules:
  0.0 46.8 jit_solution(7701266322516696768)
XLA Ops:
  0.6 0.0 copy-start
  0.6 44.3 %shard_map.58 = (bf16[576,768]{1,0:T(8,128)(2,1)S(1)}, f32[1,512]{1,0:T(1,128)S(1)}, s32[1,512]{1,0:T(1,128)S(1)}, s32[1,1]{1,0:T(1,128)}, s32[1,512]{1,0:T(1,128)S(1)}, /*index=5*/s32[1,32]{1,0:T(1,128)S(1)}) custom-call(bf16[512,768]{1,0:T(8,128)(2,1)} %emb_in.1, s32[1,512]{1,0:T(1,128)} %bitcast.9, s32[1,32]{1,0:T(1,128)} %bitcast.10), custom_call_target="tpu_custom_call" | custom-call | tf_op jit(solution)/shard_map/pallas_call | solution.py:893
  45.5 1.0 %shard_map.59 = (bf16[576,768]{1,0:T(8,128)(2,1)}, f32[1,512]{1,0:T(1,128)}, s32[1,512]{1,0:T(1,128)}) custom-call(bf16[576,768]{1,0:T(8,128)(2,1)S(1)} %get-tuple-element.55.cent_ref, f32[1,512]{1,0:T(1,128)S(1)} %get-tuple-element.56.dist_ref, s32[1,512]{1,0:T(1,128)S(1)} %get-tuple-element.57.rank_ref), custom_call_target="tpu_custom_call" | custom-call | tf_op jit(solution)/shard_map/pallas_call | solution.py:936
  46.5 0.0 copy-done
  46.5 0.2 conditional.1
Async XLA Ops:
  0.6 45.9 %copy-start = (bf16[512,768]{1,0:T(8,128)(2,1)S(1)}, bf16[512,768]{1,0:T(8,128)(2,1)}, u32[]{:S(2)}) copy-start(bf16[512,768]{1,0:T(8,128)(2,1)} %emb_in.1) | copy-start | bytes 2359300

commit v7 on v6

--- a/solution.py
+++ b/solution.py
@@ -420,7 +420,7 @@
     spots = [
         (plane, dg, dc)
         for plane in plane_order
-        for dg in range(groups)
+        for dg in list(range(1, groups)) + [0]
         for dc in range(2)
         if dg or dc or plane is not my_plane
     ]

time: 47 us -> 46.9 us (level)
  no operation moved by 1% of the time
where the time goes in v7:
time: 46.9 us; the launch traced here: 46.7 us
  Pallas kernels  45.1 us (96%)
  between operations  1.38 us (3%)
    pallas_call x1, Pallas kernels, run_fast(): pl.pallas_call(functools.partial(fast_kernel, groups, replicas, direct, s...  44.2 us
    pallas_call x1, Pallas kernels, stored(): pl.pallas_call(store_kernel, out_shape=outs[:3], in_specs=[vmem] * 3, out...  0.96 us

profile of v7, /device:TPU:0, one launch (start us, length us, event | category | flops | bytes accessed | tf_op | source)
XLA Modules:
  0.0 46.7 jit_solution(2302094683911563683)
XLA Ops:
  0.6 0.0 copy-start
  0.6 44.2 %shard_map.58 = (bf16[576,768]{1,0:T(8,128)(2,1)S(1)}, f32[1,512]{1,0:T(1,128)S(1)}, s32[1,512]{1,0:T(1,128)S(1)}, s32[1,1]{1,0:T(1,128)}, s32[1,512]{1,0:T(1,128)S(1)}, /*index=5*/s32[1,32]{1,0:T(1,128)S(1)}) custom-call(bf16[512,768]{1,0:T(8,128)(2,1)} %emb_in.1, s32[1,512]{1,0:T(1,128)} %bitcast.9, s32[1,32]{1,0:T(1,128)} %bitcast.10), custom_call_target="tpu_custom_call" | custom-call | tf_op jit(solution)/shard_map/pallas_call | solution.py:893
  45.4 1.0 %shard_map.59 = (bf16[576,768]{1,0:T(8,128)(2,1)}, f32[1,512]{1,0:T(1,128)}, s32[1,512]{1,0:T(1,128)}) custom-call(bf16[576,768]{1,0:T(8,128)(2,1)S(1)} %get-tuple-element.55.cent_ref, f32[1,512]{1,0:T(1,128)S(1)} %get-tuple-element.56.dist_ref, s32[1,512]{1,0:T(1,128)S(1)} %get-tuple-element.57.rank_ref), custom_call_target="tpu_custom_call" | custom-call | tf_op jit(solution)/shard_map/pallas_call | solution.py:936
  46.4 0.0 copy-done
  46.4 0.2 conditional.1
Async XLA Ops:
  0.6 45.7 %copy-start = (bf16[512,768]{1,0:T(8,128)(2,1)S(1)}, bf16[512,768]{1,0:T(8,128)(2,1)}, u32[]{:S(2)}) copy-start(bf16[512,768]{1,0:T(8,128)(2,1)} %emb_in.1) | copy-start | bytes 2359300
